TPU v7x, 64 devices: a 2x2x8 block of a 4x4x8 slice. The times are simulated.
64 devices in a mesh: replica: 4 (over x, y), ep: 16 (over z, core).
Axes of the slice: x: 2, y: 2, z: 8, core: 2. Of those that a mesh axis runs over, the one named last changes fastest.
The devices are a block of a 4x4x8 slice.
Arguments:
- x: bfloat16 [64, 256, 2048], P(('replica', 'ep')), parts along dimension 0
- wq: bfloat16 [2048, 4096], P('ep')
- wk: bfloat16 [2048, 4096], P('ep')
- wv: bfloat16 [2048, 4096], P('ep')
- wo: bfloat16 [4096, 2048], P('ep')
- wr: float32 [2048, 128], replicated
- w1: bfloat16 [128, 2048, 768], P('ep')
- w3: bfloat16 [128, 2048, 768], P('ep')
- w2: bfloat16 [128, 768, 2048], P('ep')
- idx: int32 [64, 256, 8], P(('replica', 'ep')), parts along dimension 0
Outputs:
- output: bfloat16 [64, 256, 2048], P(('replica', 'ep')), parts along dimension 0
There are 4 independent parts. A program takes and returns all parts, laid end to end along the dimension named above; an argument that names none is the same for every part.
All inputs are finite; a program needn't handle non-finite values.
Results may differ from a plain program's by a relative error of at most 0.0119529.
Values are sent between devices in bfloat16 or wider.
A program may use at most 768 MiB of HBM per device.

v0:
```python
import math
import jax
import jax.numpy as jnp
from jax import lax
from jax.sharding import PartitionSpec as P

HEAD = 128
BLOCK = 128
EPS = 1e-6
THETA = 10000.0


def rmsnorm(v):
    v = v.astype(jnp.float32)
    return v * lax.rsqrt(jnp.mean(v * v, axis=-1, keepdims=True) + EPS)


def rope(z):
    n = z.shape[-3]
    half = HEAD // 2
    freq = THETA ** (-jnp.arange(half, dtype=jnp.float32) / half)
    ang = jnp.arange(n, dtype=jnp.float32)[:, None] * freq
    c = jnp.cos(ang)[:, None, :]
    s = jnp.sin(ang)[:, None, :]
    z1, z2 = z[..., :half], z[..., half:]
    return jnp.concatenate([z1 * c - z2 * s, z2 * c + z1 * s], axis=-1)


def attention(x, s, wq, wk, wv, wo):
    t, d = x.shape
    nh = wq.shape[1] // HEAD
    a = rmsnorm(x).astype(jnp.bfloat16)

    def proj(w):
        return jnp.dot(a, w, preferred_element_type=jnp.float32).reshape(t // s, s, nh, HEAD)

    q = rope(proj(wq)).astype(jnp.bfloat16)
    k = rope(proj(wk)).astype(jnp.bfloat16)
    v = proj(wv).astype(jnp.bfloat16)
    sc = jnp.einsum('bqhe,bkhe->bhqk', q, k, preferred_element_type=jnp.float32) / math.sqrt(HEAD)
    sc = jnp.where(jnp.tril(jnp.ones((s, s), bool)), sc, -jnp.inf)
    p = jax.nn.softmax(sc, axis=-1).astype(jnp.bfloat16)
    o = jnp.einsum('bhqk,bkhe->bqhe', p, v, preferred_element_type=jnp.float32).astype(jnp.bfloat16)
    ao = jnp.dot(o.reshape(t, nh * HEAD), wo, preferred_element_type=jnp.float32)
    return (x.astype(jnp.float32) + ao).astype(jnp.bfloat16)


def router(h, wr, ids):
    r = rmsnorm(h)
    logits = jnp.dot(r, wr, precision=lax.Precision.HIGHEST, preferred_element_type=jnp.float32)
    g = jax.nn.softmax(jnp.take_along_axis(logits, ids, axis=1), axis=-1)
    return r.astype(jnp.bfloat16), g


def block_plan(eid, ne, cap):
    m = eid.shape[0]
    nb = (cap + ne * (BLOCK - 1)) // BLOCK + 1
    counts = jnp.bincount(eid, length=ne + 1)[:ne]
    nblk = (counts + BLOCK - 1) // BLOCK
    bend = jnp.cumsum(nblk)
    first = jnp.cumsum(counts) - counts
    order = jnp.argsort(eid)
    se = eid[order]
    sc = jnp.minimum(se, ne - 1)
    slot = jnp.where(se < ne, (bend[sc] - nblk[sc]) * BLOCK + jnp.arange(m) - first[sc], nb * BLOCK)
    cand = jnp.full((nb * BLOCK,), m, jnp.int32).at[slot].set(order.astype(jnp.int32), mode='drop')
    blk_e = jnp.minimum(jnp.searchsorted(bend, jnp.arange(nb), side='right'), ne - 1)
    return cand.reshape(nb, BLOCK), blk_e, bend[-1]


def expert_sum(rows, eid, gates, k, w1, w3, w2, cap):
    n, d = rows.shape
    ne = w1.shape[0]
    m = n * k
    cand, blk_e, nused = block_plan(eid, ne, cap)
    ok = cand < m
    row = jnp.where(ok, cand // k, 0)
    gate = jnp.where(ok, gates[jnp.minimum(cand, m - 1)], 0.0)

    def body(acc, xs):
        b, rb, gb, e = xs

        def work(acc):
            xb = rows[rb]
            a1 = jnp.dot(xb, w1[e], preferred_element_type=jnp.float32)
            a3 = jnp.dot(xb, w3[e], preferred_element_type=jnp.float32)
            act = (jax.nn.silu(a1) * a3).astype(jnp.bfloat16)
            o = jnp.dot(act, w2[e], preferred_element_type=jnp.float32).astype(jnp.bfloat16)
            return acc.at[rb].add(gb[:, None] * o.astype(jnp.float32))

        return lax.cond(b < nused, work, lambda acc: acc, acc), None

    acc, _ = lax.scan(body, jnp.zeros((n, d), jnp.float32), (jnp.arange(cand.shape[0]), row, gate, blk_e))
    return acc


def solution(mesh):
    nd = mesh.shape['ep']
    tok = P(('replica', 'ep'), None, None)
    rows_ep = P('ep', None)
    by_expert = P('ep', None, None)

    def a2a(v):
        return lax.all_to_all(v, 'ep', 0, 0, tiled=True)

    def local(x, wq, wk, wv, wo, wr, w1, w3, w2, idx):
        b, s, d = x.shape
        t, k, ne = b * s, idx.shape[-1], w1.shape[0]
        wq, wk, wv, wo = [lax.all_gather(w, 'ep', axis=0, tiled=True) for w in (wq, wk, wv, wo)]
        h = attention(x.reshape(t, d), s, wq, wk, wv, wo)
        ids = idx.reshape(t, k)
        u, g = router(h, wr, ids)
        dev = jnp.arange(nd)
        hit = jnp.any(ids[None] // ne == dev[:, None, None], axis=-1)
        pos = jnp.where(hit, jnp.cumsum(hit, axis=1) - 1, t)
        src = jnp.full((nd, t), t, jnp.int32).at[dev[:, None], pos].set(
            jnp.broadcast_to(jnp.arange(t, dtype=jnp.int32), (nd, t)), mode='drop')
        ok = src < t
        src = jnp.minimum(src, t - 1)
        mine = (ids[src] // ne == dev[:, None, None]) & ok[..., None]
        recv_x = a2a(jnp.where(ok[..., None], u[src], jnp.zeros((), jnp.bfloat16)))
        recv_e = a2a(jnp.where(mine, ids[src] % ne, ne))
        recv_g = a2a(jnp.where(mine, g[src], 0.0))
        n = nd * t
        part = expert_sum(recv_x.reshape(n, d), recv_e.reshape(-1), recv_g.reshape(-1), k,
                          w1, w3, w2, n * min(k, ne))
        back = a2a(part.astype(jnp.bfloat16).reshape(nd, t, d))
        moe = jnp.zeros((t, d), jnp.float32).at[src].add(
            jnp.where(ok[..., None], back.astype(jnp.float32), 0.0))
        return (h.astype(jnp.float32) + moe).astype(jnp.bfloat16).reshape(b, s, d)

    return jax.shard_map(local, mesh=mesh,
                         in_specs=(tok, rows_ep, rows_ep, rows_ep, rows_ep, P(None, None),
                                   by_expert, by_expert, by_expert, tok),
                         out_specs=tok, check_vma=False)
```

profile of v0, /device:TPU:21, one launch (start us, length us, event | category | flops | bytes accessed | tf_op | source)
XLA Modules:
  0.0 7564.5 jit_solution(9764949401783368608)
XLA Ops:
  11.0 15.5 scatter_custom_fusion.4
  52.7 56.1 all-gather.9.cloned.1.call-done
  108.9 22.5 copy.50
  131.4 69.7 all-gather.7.cloned.1.call-done
  201.1 22.4 copy.49
  223.5 69.8 all-gather.5.cloned.1.call-done
  293.3 22.3 copy.48
  354.2 31.2 all-gather.11.cloned.1.call-done
  411.1 21.0 gather_fusion.5
  448.9 14.0 broadcast_select_fusion
  484.8 180.7 %gather_fusion.2 = s32[32768]{0:T(1024)S(1)} fusion(s32[32768]{0:T(1024)S(1)} %reshape.434, s32[32768]{0:T(1024)S(1)} %fusion.84), kind=kCustom, calls=%fused_computation.2 | custom fusion | bytes 393216 | tf_op jit(solution)/shard_map/gather | solution.py:63
  668.1 226.3 %scatter_custom_fusion.1 = s32[9]{0:T(128)S(1)} fusion(s32[32768]{0:T(1024)S(1)} %reshape.578, s32[32768]{0:T(1024)S(1)} %broadcast.479, s32[]{:T(128)} %copy.96), kind=kCustom, calls=%fused_computation.192 | custom fusion | flops 32768 | bytes 40 | tf_op jit(solution)/shard_map/scatter-add | solution.py:58
  913.2 120.1 %scatter_custom_fusion.2 = s32[33792]{0:T(1024)S(1)} fusion(s32[32768]{0:T(1024)S(1)} %bitcast.235, s32[32768]{0:T(1024)S(1)} %get-tuple-element.210, s32[]{:T(128)} %constant.195.clone.1), kind=kCustom, calls=%fused_computation.138 | custom fusion | bytes 135172 | tf_op jit(solution)/shard_map/scatter | solution.py:66
  1033.3 22.7 while.38
  1057.8 186.2 %gather_fusion.4 = f32[33792]{0:T(1024)S(1)} fusion(f32[32768]{0:T(1024)S(1)} %reshape.440, s32[33792]{0:T(1024)S(1)} %fusion.79), kind=kCustom, calls=%fused_computation.4 | custom fusion | bytes 405504 | tf_op jit(solution)/shard_map/gather | solution.py:78
  1255.2 1147.8 %while.37 = (s32[]{:T(128)}, f32[4096,2048]{1,0:T(8,128)}, s32[264]{0:T(512)S(1)}, s32[]{:T(128)}, s32[264,128]{1,0:T(8,128)S(1)}, /*index=5*/f32[264,128]{1,0:T...) while((s32[]{:T(128)}, f32[4096,2048]{1,0:T(8,128)}, ...), condition=%wide.region_21.22_spmd, body=%wide.region_17.21_spmd.sunk | while | flops 1209599360 | bytes 16524569 | solution.py:93
  1257.1 42.1 conditional.2
  1275.5 23.7 scatter_fusion
  1301.1 42.1 conditional.2
  1319.5 23.7 scatter_fusion
  1345.1 42.1 conditional.2
  1363.5 23.7 scatter_fusion
  1389.1 42.1 conditional.2
  1407.5 23.7 scatter_fusion
  1433.1 42.1 conditional.2
  1451.5 23.7 scatter_fusion
  1477.1 42.1 conditional.2
  1495.5 23.7 scatter_fusion
  1521.1 42.1 conditional.2
  1539.5 23.7 scatter_fusion
  1565.1 42.1 conditional.2
  1583.4 23.7 scatter_fusion
  1609.1 42.1 conditional.2
  1627.4 23.7 scatter_fusion
  1653.1 42.1 conditional.2
  1671.4 23.7 scatter_fusion
  1697.0 42.1 conditional.2
  1715.4 23.7 scatter_fusion
  1741.0 42.1 conditional.2
  1759.4 23.7 scatter_fusion
  1785.0 42.1 conditional.2
  1803.4 23.7 scatter_fusion
  1829.0 42.1 conditional.2
  1847.4 23.7 scatter_fusion
  1873.0 42.1 conditional.2
  1891.4 23.7 scatter_fusion
  2415.1 5077.4 %all_to_all.20 = bf16[16,256,2048]{2,1,0:T(8,128)(2,1)S(1)} all-to-all(bf16[16,256,2048]{2,1,0:T(8,128)(2,1)S(1)} %bitcast.216), channel_id=1, replica_groups=mesh['replica'=4,'ep'=16] {'ep'}, dimensions={0} | all-to-all | bytes 33554432 | tf_op jit(solution)/shard_map/all_to_all | solution.py:104
  7503.6 53.0 scatter_fusion.1
  (762 shorter events, 620.3 us)
Async XLA Ops:
  6.5 389.0 %copy-start = (f32[2048,128]{1,0:T(8,128)S(1)}, f32[2048,128]{1,0:T(8,128)}, u32[]{:S(2)}) copy-start(f32[2048,128]{1,0:T(8,128)} %param.21) | copy-start | bytes 3145732
  6.6 4.2 copy-start.15
  6.6 4.3 copy-start.14
  6.6 3.0 copy-start.13
  6.6 102.3 %all-gather.9.cloned.1.call-start = ((), (), s32[]{:S(2)}) async-start(), calls=%async_computation.6 | async-start | bytes 17825792 | tf_op jit(solution)/shard_map/all_gather | solution.py:109
  7.3 193.7 %all-gather.7.cloned.1.call-start = ((), (), s32[]{:S(2)}) async-start(), calls=%async_computation.5 | async-start | bytes 17825792 | tf_op jit(solution)/shard_map/all_gather | solution.py:109
  8.2 285.1 %all-gather.5.cloned.1.call-start = ((), (), s32[]{:S(2)}) async-start(), calls=%async_computation.4 | async-start | bytes 17825792 | tf_op jit(solution)/shard_map/all_gather | solution.py:109
  9.0 376.4 %all-gather.11.cloned.1.call-start = ((), (), s32[]{:S(2)}) async-start(), calls=%async_computation.7 | async-start | bytes 17825792 | tf_op jit(solution)/shard_map/all_gather | solution.py:109
  26.6 0.6 copy-start.8
  26.6 11.9 copy-start.10
  38.5 92.9 %copy-start.6 = (s32[16,256,8]{1,2,0:T(8,128)}, s32[16,256,8]{1,2,0:T(8,128)S(1)}, u32[]{:S(2)}) copy-start(s32[16,256,8]{1,2,0:T(8,128)S(1)} %copy.58) | copy-start | bytes 393220
  39.3 404.9 %all-to-all-start = ((s32[16,256,8]{1,2,0:T(8,128)}), s32[16,256,8]{1,2,0:T(8,128)}, u32[]{:S(2)}, u32[]{:S(2)}) async-start(s32[16,256,8]{1,2,0:T(8,128)} %fusion.83), calls=%async_computation | async-start | bytes 262144 | tf_op jit(solution)/shard_map/all_to_all | solution.py:104
  293.3 22.3 copy-start.5
  315.6 10.5 copy-start.4
  394.3 1.3 copy-start.2
  432.1 11.3 copy-start.7
  432.1 11.3 copy-start.11
  444.2 18.7 all-to-all-start.1
  463.0 781.0 %all-to-all-start.2 = ((bf16[16,256,2048]{2,1,0:T(8,128)(2,1)}), bf16[16,256,2048]{2,1,0:T(8,128)(2,1)}, u32[]{:S(2)}, u32[]{:S(2)}) async-start(bf16[16,256,2048]{2,1,0:T(8,128)(2,1)} %broadcast_select_fusion), calls=%async_computation.2 | async-start | bytes 33554432 | tf_op jit(solution)/shard_map/all_to_all | solution.py:104
  2415.1 5077.4 %copy-start.12 = (pred[16,256]{1,0:T(8,128)(4,1)S(1)}, pred[16,256]{1,0:T(8,128)(4,1)}, u32[]{:S(2)}) copy-start(pred[16,256]{1,0:T(8,128)(4,1)} %copy-done.10) | copy-start | bytes 12292
  7492.5 11.1 copy-start.3
  7492.5 11.1 copy-start.9
  7503.6 54.1 copy-start.1
Sparse Core Ops, SparseCore 0:
  9.0 99.8 all-gather.8
  110.5 90.5 all-gather.6
  202.7 90.5 all-gather.4
  294.8 90.5 all-gather.10
where the time goes:
time: 7660 us; the launch traced here: 7560 us
  blocking collectives  5080 us (66%)
  local copies, waits for them, and re-layouts  956 us (12%)
  other arithmetic  736 us (10%)
  loops' own time  389 us (5%)
  waiting for transfers between devices  230 us (3%)
  matrix products  138 us (2%)
    all_to_all x1, blocking collectives, a2a(): return lax.all_to_all(v, 'ep', 0, 0, tiled=True)  5080 us
    another operation x1, loops' own time, expert_sum(): lax.scan(body, jnp.zeros((n, d), jnp.float32), (jnp.arange(cand.shape[0])...  360 us
    scatter-add x15, other arithmetic, work(): return acc.at[rb].add(gb[:, None] * o.astype(jnp.float32))  355 us
    all_gather x4, waiting for transfers between devices, local(): lax.all_gather(w, 'ep', axis=0, tiled=True)  227 us
    scatter-add x1, other arithmetic, block_plan(): counts = jnp.bincount(eid, length=ne + 1)[:ne]  226 us
    gather x1, local copies, waits for them, and re-layouts, expert_sum(): gate = jnp.where(ok, gates[jnp.minimum(cand, m - 1)], 0.0)  186 us
    gather x1, local copies, waits for them, and re-layouts, block_plan(): se = eid[order]  181 us
    dynamic_slice x279, local copies, waits for them, and re-layouts, expert_sum(): lax.scan(body, jnp.zeros((n, d), jnp.float32), (jnp.arange(cand.shape[0])...  164 us
  transfers between devices with their start and end apart: 7, of which 4 were waited for; matrix products, arithmetic and copies ran while one was open for 13% of the time, Pallas kernels for 0%

commit v1 on v0

v1 whole, which is shorter than its diff:
```python
import functools
import math
import jax
import jax.numpy as jnp
from jax import lax
from jax.experimental import pallas as pl
from jax.experimental.pallas import tpu as pltpu
from jax.sharding import PartitionSpec as P

HEAD = 128
EPS = 1e-6
THETA = 10000.0
BLK = 256
SPM = 128
DENSE_AT = 32
LANES = 128
CHUNKS = 2


def rmsnorm(v):
    v = v.astype(jnp.float32)
    return v * lax.rsqrt(jnp.mean(v * v, axis=-1, keepdims=True) + EPS)


def attention_kernel(x_hbm, idx_hbm, wq_hbm, wk_hbm, wv_hbm, wo_hbm, cos_ref, sin_ref, h_ref, idx_ref,
                     xall, wqkv, stage, wov, obuf, orecv, acc, lsem, xs_s, xs_r, ix_s, ix_r, wa_s, wa_r, wb_s, wb_r,
                     wd_s, wd_r, oz_s, oz_r, oxy_s, oxy_r, od_s, od_r, oo_s, oo_r, *, nr, ne):
    side = math.isqrt(nr)
    nz = ne // 2
    far = nz // 2
    s, d = x_hbm.shape
    wrows, cols = wqkv.shape[1] // ne, wqkv.shape[2]
    orows = wov.shape[1] // 2
    quart = s // 4
    piece = orows // 4
    r, e = lax.axis_index('replica'), lax.axis_index('ep')
    z, c = e // 2, e % 2
    px, py = r // side, r % side
    qx, qy = px % 2, py % 2
    q = 2 * qx + qy
    me = 2 * q + c
    par = (qx + qy) % 2
    rx = r + side * (1 - 2 * qx)
    ry = r + (1 - 2 * qy)
    rd = rx + (1 - 2 * qy)
    jx, jy, jd = 2 * (1 - qx) + qy, 2 * qx + (1 - qy), 2 * (1 - qx) + (1 - qy)
    ep_other = 2 * z + 1 - c
    ring = (2 * ((z + 1) % nz) + c, 2 * ((z + nz - 1) % nz) + c)

    def quad(j):
        return (px - qx + j // 2) * side + (py - qy + j % 2)

    def came(way, dist):
        return (z + nz - dist) % nz if way == 0 else (z + dist) % nz

    def remote(src, dst, ssem, rsem, rep, ep):
        return pltpu.make_async_remote_copy(src_ref=src, dst_ref=dst, send_sem=ssem, recv_sem=rsem,
                                            device_id={'replica': rep, 'ep': ep}, device_id_type=pl.DeviceIdType.MESH)

    def al(v, m):
        return pl.multiple_of(v, m)

    loads = [pltpu.make_async_copy(x_hbm, xall.at[me], lsem.at[0])]
    for w, ref in enumerate((wq_hbm, wk_hbm, wv_hbm)):
        loads.append(pltpu.make_async_copy(ref.at[:, pl.ds(al(me * cols, cols), cols)],
                                           wqkv.at[w, pl.ds(al(e * wrows, wrows), wrows)], lsem.at[1 + w]))
        loads.append(pltpu.make_async_copy(ref.at[:, pl.ds(al((2 * q + 1 - c) * cols, cols), cols)],
                                           stage.at[w, z], lsem.at[4 + w]))
    loads.append(pltpu.make_async_copy(wo_hbm, wov.at[z, pl.ds(al(c * orows, orows), orows)], lsem.at[7]))
    loads.append(pltpu.make_async_copy(idx_hbm.at[q], idx_ref.at[q], lsem.at[8]))
    for cp in loads:
        cp.start()

    barrier = pltpu.get_barrier_semaphore()
    peers = [(rx, e), (ry, e), (rd, e), (r, ep_other), (rx, ep_other), (ry, ep_other), (rd, ep_other), (r, ring[0]), (r, ring[1])]
    for rep, ep in peers:
        pl.semaphore_signal(barrier, inc=1, device_id={'replica': rep, 'ep': ep}, device_id_type=pl.DeviceIdType.MESH)
    pl.semaphore_wait(barrier, len(peers))
    for cp in loads:
        cp.wait()

    sends = []

    def go(*a):
        cp = remote(*a)
        cp.start()
        sends.append(cp)

    def part_a(zz):
        return wqkv.at[:, pl.ds(al((2 * zz + c) * wrows, wrows), wrows)]

    def part_b(zz):
        return stage.at[:, zz]

    def send_w(zz, way, dist):
        if dist <= far - way:
            go(part_a(zz), part_a(zz), wa_s.at[way, dist - 1], wa_r.at[way, dist - 1], r, ring[way])
        if dist <= far - 1 + way:
            go(part_b(zz), part_b(zz), wb_s.at[way, dist - 1], wb_r.at[way, dist - 1], r, ring[way])

    def cross_w(zz, k):
        go(part_b(zz), part_a(zz), wd_s.at[k], wd_r.at[zz], r, ep_other)

    for way in range(2):
        send_w(z, way, 1)
    for rep, k in ((rx, 0), (ry, 1), (rd, 2)):
        go(xall.at[me], xall.at[me], xs_s.at[k], xs_r.at[me], rep, e)
    cross_w(z, 0)
    go(xall.at[me], xall.at[me], xs_s.at[3], xs_r.at[me], r, ep_other)
    for k in range(4):
        @pl.when(q != k)
        def _():
            remote(idx_hbm.at[k], idx_ref.at[q], ix_s.at[k], ix_r.at[q], quad(k), e).start()

    def wait_w(dist):
        for way in range(2):
            zz = came(way, dist)
            if dist <= far - way:
                remote(part_a(zz), part_a(zz), wa_s.at[way, dist - 1], wa_r.at[way, dist - 1], r, e).wait_recv()
                if dist + 1 <= far - way:
                    go(part_a(zz), part_a(zz), wa_s.at[way, dist], wa_r.at[way, dist], r, ring[way])
            if dist <= far - 1 + way:
                remote(part_b(zz), part_b(zz), wb_s.at[way, dist - 1], wb_r.at[way, dist - 1], r, e).wait_recv()
                if dist + 1 <= far - 1 + way:
                    go(part_b(zz), part_b(zz), wb_s.at[way, dist], wb_r.at[way, dist], r, ring[way])
                cross_w(zz, 1 + 2 * (dist - 1) + way if dist < far else nz - 1)

    def pass_x(j, k):
        at = xall.at[2 * j + c]
        remote(at, at, xs_s.at[k], xs_r.at[2 * j + c], r, e).wait_recv()
        go(at, at, xs_s.at[k], xs_r.at[2 * j + c], r, ep_other)

    def half_piece(zz, h, p):
        return wov.at[zz, pl.ds(al(c * orows + 2 * piece * p + piece * h, piece), piece)]

    def send_o_ring(zz, h, way, i):
        go(half_piece(zz, h, par), half_piece(zz, h, par), oz_s.at[way, i], oz_r.at[way, i], r, ring[way])

    steps = 2 * (far - 1) + 1

    def order(way, i):
        return (1 + i // 2, i % 2) if i < steps - 1 else (far, way)

    def serve(i):
        for way in range(2):
            dist, h = order(way, i)
            zz = came(way, dist)
            at = half_piece(zz, h, par)
            remote(at, at, oz_s.at[way, i], oz_r.at[way, i], r, e).wait_recv()
            if i + 2 < steps - 1:
                send_o_ring(zz, h, way, i + 2)
            elif dist == far - 1 and h == way:
                send_o_ring(zz, h, way, steps - 1)
            go(at, at, oxy_s.at[way, i], oxy_r.at[way, i], rx if h == 0 else ry, e)
            go(at, at, od_s.at[way, i], od_r.at[zz], r, ep_other)

    def serve_side(i):
        for way in range(2):
            dist, h = order(way, i)
            zz = came(way, dist)
            at = half_piece(zz, h, 1 - par)
            remote(at, at, oxy_s.at[way, i], oxy_r.at[way, i], r, e).wait_recv()
            go(at, at, od_s.at[2 + way, i], od_r.at[zz], r, ep_other)

    for dist in range(1, far):
        wait_w(dist)
        if dist == max(1, far - 2):
            pass_x(jx, 4)
            pass_x(jy, 5)
    for h in range(2):
        for way in range(2):
            send_o_ring(z, h, way, h)
    own = wov.at[z, pl.ds(al(c * orows, orows), orows)]
    go(own, own, od_s.at[4, 0], od_r.at[z], r, ep_other)
    pass_x(jd, 6)
    wait_w(far)
    for zz in range(nz):
        at = wqkv.at[:, pl.ds((2 * zz + 1 - c) * wrows, wrows)]
        remote(at, at, wd_s.at[0], wd_r.at[zz], r, e).wait_recv()
    for j in range(4):
        at = xall.at[2 * j + 1 - c]
        remote(at, at, xs_s.at[0], xs_r.at[2 * j + 1 - c], r, e).wait_recv()

    nh = cols // HEAD
    scale = 1.0 / math.sqrt(HEAD)

    def send_o(t):
        j, cc = t // 2, t % 2
        for k in range(4):
            src = obuf.at[t, pl.ds(quart * k, quart)]
            dst = orecv.at[me, pl.ds(al(quart * j, quart), quart)]

            @pl.when((q != k) | (c != cc))
            def _():
                remote(src, dst, oo_s.at[t, k], oo_r.at[me], quad(k), 2 * z + cc).start()

            @pl.when((q == k) & (c == cc))
            def _():
                dst[...] = src[...]

    def sequence(t, _):
        xf = xall[t].astype(jnp.float32)
        a = (xf * lax.rsqrt(jnp.mean(xf * xf, axis=-1, keepdims=True) + EPS)).astype(jnp.bfloat16)
        qf = jnp.dot(a, wqkv[0], preferred_element_type=jnp.float32)
        kf = jnp.dot(a, wqkv[1], preferred_element_type=jnp.float32)
        vf = jnp.dot(a, wqkv[2], preferred_element_type=jnp.float32)
        cs, sn = cos_ref[...], sin_ref[...]
        row = lax.broadcasted_iota(jnp.int32, (s, s), 0)
        col = lax.broadcasted_iota(jnp.int32, (s, s), 1)
        for n in range(nh):
            at = slice(n * HEAD, (n + 1) * HEAD)
            qh, kh = qf[:, at], kf[:, at]
            qh = (qh * cs + pltpu.roll(qh, HEAD // 2, 1) * sn).astype(jnp.bfloat16)
            kh = (kh * cs + pltpu.roll(kh, HEAD // 2, 1) * sn).astype(jnp.bfloat16)
            sc = lax.dot_general(qh, kh, (((1,), (1,)), ((), ())), preferred_element_type=jnp.float32) * scale
            sc = jnp.where(row >= col, sc, -1e30)
            p = jnp.exp(sc - jnp.max(sc, axis=-1, keepdims=True))
            p = (p * (1.0 / jnp.sum(p, axis=-1, keepdims=True))).astype(jnp.bfloat16)
            obuf[t, :, at] = jnp.dot(p, vf[:, at].astype(jnp.bfloat16), preferred_element_type=jnp.float32).astype(jnp.bfloat16)

        @pl.when(t > 0)
        def _():
            send_o(t - 1)
        return 0

    lax.fori_loop(0, 4, sequence, 0)
    serve(0)
    lax.fori_loop(4, 8, sequence, 0)
    serve(1)
    serve_side(0)
    send_o(7)
    serve(2)
    serve_side(1)

    for k in range(8):
        @pl.when(k != me)
        def _():
            at = orecv.at[k]
            remote(at, at, oo_s.at[0, 0], oo_r.at[k], r, e).wait_recv()

    for j in range(4):
        acc[pl.ds(quart * j, quart), :] = xall[2 * j + c, pl.ds(al(quart * q, quart), quart), :].astype(jnp.float32)

    def project(zz):
        at = wov.at[zz, pl.ds(al((1 - c) * orows, orows), orows)]
        remote(at, at, od_s.at[0, 0], od_r.at[zz], r, e).wait_recv()
        width = min(512, d)

        def chunk(n, _):
            cut = pl.ds(al(n * width, width), width)
            acc[:, cut] = acc[:, cut] + jnp.dot(orecv[zz], wov[zz, :, cut], preferred_element_type=jnp.float32)
            return 0

        lax.fori_loop(0, d // width, chunk, 0)

    project(z)
    for i in range(3, steps):
        serve(i)
        serve_side(i - 1)
        if i % 2 == 1 and i // 2 < far:
            for way in range(2):
                project(came(way, i // 2))
    serve_side(steps - 1)
    for way in range(2):
        project(came(way, far - 1))
    project(came(0, far))
    h_ref[...] = acc[...].astype(jnp.bfloat16)
    for k in range(4):
        @pl.when(q != k)
        def _():
            remote(idx_hbm.at[k], idx_ref.at[k], ix_s.at[k], ix_r.at[k], r, e).wait()
    for t in range(8):
        for k in range(4):
            src = obuf.at[t, pl.ds(quart * k, quart)]

            @pl.when((q != k) | (c != t % 2))
            def _():
                remote(src, src, oo_s.at[t, k], oo_r.at[0], r, e).wait_send()
    for cp in sends:
        cp.wait_send()


def attention_call(x, idx, wq, wk, wv, wo, nr, ne):
    s, d = x.shape
    hd = wq.shape[1]
    cols = hd // 8
    nz = ne // 2
    steps = nz - 1
    half = HEAD // 2
    freq = THETA ** (-jnp.arange(half, dtype=jnp.float32) / half)
    ang = jnp.arange(s, dtype=jnp.float32)[:, None] * freq
    cos, sin = jnp.cos(ang), jnp.sin(ang)
    cos = jnp.concatenate([cos, cos], axis=1)
    sin = jnp.concatenate([-sin, sin], axis=1)
    any_ = pl.BlockSpec(memory_space=pl.ANY)
    vmem = pl.BlockSpec(memory_space=pltpu.VMEM)
    bf = jnp.bfloat16
    dma = pltpu.SemaphoreType.DMA
    return pl.pallas_call(
        functools.partial(attention_kernel, nr=nr, ne=ne),
        out_shape=(jax.ShapeDtypeStruct((s, d), bf), jax.ShapeDtypeStruct(idx.shape, idx.dtype)),
        in_specs=[any_, any_, any_, any_, any_, any_, vmem, vmem],
        out_specs=(vmem, vmem),
        scratch_shapes=[
            pltpu.VMEM((8, s, d), bf),
            pltpu.VMEM((3, d, cols), bf),
            pltpu.VMEM((3, nz, d // ne, cols), bf),
            pltpu.VMEM((nz, 2 * wo.shape[0], d), bf),
            pltpu.VMEM((8, s, cols), bf),
            pltpu.VMEM((8, s, cols), bf),
            pltpu.VMEM((s, d), jnp.float32),
            dma((9,)), dma((7,)), dma((8,)), dma((4,)), dma((4,)),
            dma((2, nz // 2)), dma((2, nz // 2)), dma((2, nz // 2)), dma((2, nz // 2)),
            dma((nz,)), dma((nz,)),
            dma((2, steps)), dma((2, steps)), dma((2, steps)), dma((2, steps)),
            dma((5, steps)), dma((nz,)), dma((8, 4)), dma((8,)),
        ],
        compiler_params=pltpu.CompilerParams(collective_id=0, has_side_effects=True, vmem_limit_bytes=60 * 2**20),
        cost_estimate=pl.CostEstimate(flops=100 * 10**9, bytes_accessed=30 * 10**6, transcendentals=10**6),
        name='attention',
    )(x, idx, wq, wk, wv, wo, cos, sin)


def router(h, wr, ids):
    r = rmsnorm(h)
    logits = jnp.dot(r, wr, precision=lax.Precision.HIGHEST, preferred_element_type=jnp.float32)
    hot = ids[:, :, None] == jnp.arange(wr.shape[1], dtype=jnp.int32)
    picked = jnp.sum(jnp.where(hot, logits[:, None, :], 0.0), axis=-1)
    return r.astype(jnp.bfloat16), jax.nn.softmax(picked, axis=-1)


def expert_kernel(nsp_ref, dense_ref, list_ref, glist_ref, gate_ref, u_hbm, w1, w3, w2, out_hbm,
                  u3, acc, ubuf, wup, wdown, act, xs, zs, sems, *, cap, run):
    ne, d, f = w1.shape
    t = u_hbm.shape[0]
    nb = t // BLK
    seg = d // LANES
    per = BLK // run
    ndev = t // (4 * run)

    def fetch(slot, e):
        pltpu.make_async_copy(w1.at[e], wup.at[slot, 0], sems.at[slot, 0]).start()
        pltpu.make_async_copy(w3.at[e], wup.at[slot, 1], sems.at[slot, 1]).start()
        pltpu.make_async_copy(w2.at[e], wdown.at[slot], sems.at[slot, 2]).start()

    def load(b):
        b = jnp.asarray(b, jnp.int32)
        j, first = b // (nb // 4), (b % (nb // 4)) * per
        for k in range(per):
            src = u_hbm.at[pl.ds(pl.multiple_of(((first + k) * 4 + j) * run, run), run)]
            pltpu.make_async_copy(src, ubuf.at[b % 2, pl.ds(k * run, run)], sems.at[2, b % 2]).start()

    load(0)
    load(1)
    fetch(0, 0)
    acc[...] = jnp.zeros_like(acc)
    u3[pl.ds(t * seg, seg), :] = jnp.zeros((seg, LANES), jnp.float32)

    def widen(b, _):
        at = ubuf.at[b % 2]
        pltpu.make_async_copy(at, at, sems.at[2, b % 2]).wait()
        for j in range(seg):
            u3[pl.ds(b * BLK * seg + j, BLK, stride=seg), :] = at[:, j * LANES:(j + 1) * LANES].astype(jnp.float32)

        @pl.when(b + 2 < nb)
        def _():
            load(b + 2)
        return 0

    lax.fori_loop(0, nb, widen, 0)
    x = ubuf.at[0]

    def hidden(slot, rows):
        for c in range(0, f, BLK):
            a1 = jnp.dot(x[:rows, :], wup[slot, 0, :, c:c + BLK], preferred_element_type=jnp.float32)
            a3 = jnp.dot(x[:rows, :], wup[slot, 1, :, c:c + BLK], preferred_element_type=jnp.float32)
            act[:rows, c:c + BLK] = (jax.nn.silu(a1) * a3).astype(jnp.bfloat16)

    def expert(e, _):
        slot = lax.rem(e, 2)

        @pl.when(e + 1 < ne)
        def _():
            fetch(1 - slot, e + 1)

        for j in range(2):
            pltpu.make_async_copy(wup.at[slot, j], wup.at[slot, j], sems.at[slot, j]).wait()
        pltpu.make_async_copy(wdown.at[slot], wdown.at[slot], sems.at[slot, 2]).wait()

        def block(b, _):
            @pl.when(dense_ref[e * nb + b] != 0)
            def _():
                r0 = pl.multiple_of(b * BLK, BLK)
                for j in range(seg):
                    x[:, j * LANES:(j + 1) * LANES] = u3[pl.ds(r0 * seg + j, BLK, stride=seg), :].astype(jnp.bfloat16)
                hidden(slot, BLK)
                lane = lax.broadcasted_iota(jnp.int32, (BLK, LANES), 1)
                g = jnp.sum(jnp.where(lane == e, gate_ref[pl.ds(r0, BLK), :], 0.0), axis=1, keepdims=True)
                for c in range(0, d, 2 * BLK):
                    z = jnp.dot(act[...], wdown[slot, :, c:c + 2 * BLK], preferred_element_type=jnp.float32)
                    z = z.astype(jnp.bfloat16).astype(jnp.float32)
                    z = jnp.where(g != 0.0, g * z, 0.0)
                    for j in range(2 * BLK // LANES):
                        at = pl.ds(r0 * seg + c // LANES + j, BLK, stride=seg)
                        acc[at, :] = acc[at, :] + z[:, j * LANES:(j + 1) * LANES]
            return 0

        lax.fori_loop(0, nb, block, 0)
        n = nsp_ref[e]

        def tile(i, _):
            base = e * cap + i * SPM
            groups = (jnp.minimum(n - i * SPM, SPM) + 7) // 8

            def gather(q, _):
                for s in range(8):
                    tok = list_ref[base + q * 8 + s]
                    xs[pl.ds(pl.multiple_of((q * 8 + s) * seg, seg), seg), :] = u3[pl.ds(pl.multiple_of(tok * seg, seg), seg), :]
                return 0

            lax.fori_loop(0, groups, gather, 0)
            for j in range(seg):
                x[:SPM, j * LANES:(j + 1) * LANES] = xs[pl.ds(j, SPM, stride=seg), :].astype(jnp.bfloat16)
            hidden(slot, SPM)
            for c in range(0, d, 2 * BLK):
                z = jnp.dot(act[:SPM, :], wdown[slot, :, c:c + 2 * BLK], preferred_element_type=jnp.float32)
                z = z.astype(jnp.bfloat16).astype(jnp.float32)
                for j in range(2 * BLK // LANES):
                    zs[pl.ds(c // LANES + j, SPM, stride=seg), :] = z[:, j * LANES:(j + 1) * LANES]

            def scatter(q, _):
                for s in range(8):
                    tok = list_ref[base + q * 8 + s]
                    g = glist_ref[base + q * 8 + s]
                    at = pl.ds(pl.multiple_of(tok * seg, seg), seg)
                    acc[at, :] = acc[at, :] + g * zs[pl.ds(pl.multiple_of((q * 8 + s) * seg, seg), seg), :]
                return 0

            lax.fori_loop(0, groups, scatter, 0)
            return 0

        lax.fori_loop(0, (n + SPM - 1) // SPM, tile, 0)
        return 0

    lax.fori_loop(0, ne, expert, 0)

    def store(k, _):
        for j in range(4):
            src = acc.at[pl.ds(pl.multiple_of((j * ndev + k) * run * seg, run * seg), run * seg)]
            dst = out_hbm.at[pl.ds(pl.multiple_of((k * 4 + j) * run * seg, run * seg), run * seg)]
            pltpu.make_async_copy(src, dst, sems.at[2, 2]).start()
        return 0

    lax.fori_loop(0, ndev, store, 0)
    pltpu.make_async_copy(acc.at[pl.ds(0, t * seg)], out_hbm, sems.at[2, 2]).wait()


def expert_call(u, gates, nsp, dense, rows, glist, w1, w3, w2, run):
    t, d = u.shape
    ne, _, f = w1.shape
    cap = rows.shape[0] // ne
    seg = d // LANES
    any_ = pl.BlockSpec(memory_space=pl.ANY)
    smem = pl.BlockSpec(memory_space=pltpu.SMEM)
    return pl.pallas_call(
        functools.partial(expert_kernel, cap=cap, run=run),
        out_shape=jax.ShapeDtypeStruct((t * seg, LANES), jnp.float32),
        in_specs=[smem] * 4 + [pl.BlockSpec(memory_space=pltpu.VMEM)] + [any_] * 4,
        out_specs=any_,
        scratch_shapes=[
            pltpu.VMEM(((t + 1) * seg, LANES), jnp.float32),
            pltpu.VMEM(((t + 1) * seg, LANES), jnp.float32),
            pltpu.VMEM((2, BLK, d), jnp.bfloat16),
            pltpu.VMEM((2, 2, d, f), jnp.bfloat16),
            pltpu.VMEM((2, f, d), jnp.bfloat16),
            pltpu.VMEM((BLK, f), jnp.bfloat16),
            pltpu.VMEM((SPM * seg, LANES), jnp.float32),
            pltpu.VMEM((SPM * seg, LANES), jnp.float32),
            pltpu.SemaphoreType.DMA((3, 3)),
        ],
        compiler_params=pltpu.CompilerParams(vmem_limit_bytes=62 * 2**20),
        cost_estimate=pl.CostEstimate(flops=60 * 10**9, bytes_accessed=160 * 10**6, transcendentals=10**6),
        name='experts',
    )(nsp, dense, rows, glist, gates, u, w1, w3, w2)


def plan(ids, g, eids):
    t = ids.shape[0]
    ne = eids.shape[0]
    nb = t // BLK
    cap = nb * DENSE_AT
    eq = ids[:, :, None] == eids
    gates = jnp.sum(jnp.where(eq, g[:, :, None], 0.0), axis=1)
    m = jnp.any(eq, axis=1)
    dense = jnp.sum(m.reshape(nb, BLK, ne), axis=1, dtype=jnp.int32) >= DENSE_AT
    sp = m & ~jnp.repeat(dense, BLK, axis=0)
    spb = sp.astype(jnp.bfloat16).reshape(t // LANES, LANES, ne)
    tri = (jnp.arange(LANES)[None, :] < jnp.arange(LANES)[:, None]).astype(jnp.bfloat16)
    inner = jnp.einsum('ij,bje->bie', tri, spb, preferred_element_type=jnp.float32)
    tot = jnp.sum(spb.astype(jnp.float32), axis=1)
    nt = t // LANES
    before = jnp.sum(jnp.where((jnp.arange(nt)[None, :] < jnp.arange(nt)[:, None])[:, :, None], tot[None], 0.0), axis=1)
    pos = (inner + before[:, None, :]).reshape(t, ne).astype(jnp.int32)
    pos = jnp.where(sp, pos, -1)
    nsp = jnp.sum(sp, axis=0, dtype=jnp.int32)
    at = pos.T[:, None, :] == jnp.arange(cap)[None, :, None]
    rows = jnp.sum(jnp.where(at, jnp.arange(t)[None, None, :] - t, 0), axis=-1, dtype=jnp.int32) + t
    glist = jnp.sum(jnp.where(at, gates.T[:, None, :], 0.0), axis=-1)
    gates = jnp.pad(gates, ((0, 0), (0, LANES - ne)))
    return gates, nsp, dense.T.reshape(-1).astype(jnp.int32), rows.reshape(-1), glist.reshape(-1)


def solution(mesh):
    nr, nd = mesh.shape['replica'], mesh.shape['ep']
    side = math.isqrt(nr)
    tok = P(('replica', 'ep'), None, None)
    rows_ep = P('ep', None)
    by_expert = P('ep', None, None)
    quads = [[(bx + j // 2) * side + by + j % 2 for j in range(4)] for bx in range(0, side, 2) for by in range(0, side, 2)]

    def local(x, wq, wk, wv, wo, wr, w1, w3, w2, idx):
        b, s, d = x.shape
        t, k, ne = b * s, idx.shape[-1], w1.shape[0]
        me = lax.axis_index('ep')
        quart = t // 4
        own = jnp.pad(idx.reshape(t, k), ((0, 0), (0, LANES - k))).reshape(4, quart, LANES)
        h, ids = attention_call(x.reshape(t, d), own, wq, wk, wv, wo, nr, nd)
        ids = ids.reshape(t, LANES)[:, :k]
        u, g = router(h, wr, ids)
        run = quart // CHUNKS
        u4, h4 = u.reshape(4, quart, d), h.reshape(4, quart, d)
        us = [lax.all_gather(u4[:, i * run:(i + 1) * run].reshape(4 * run, d), 'ep', axis=0, tiled=True) for i in range(CHUNKS)]
        gi = lax.all_gather(jnp.concatenate([g, ids.astype(jnp.float32)], axis=1), 'ep', axis=0, tiled=False)
        gi = gi.reshape(nd, 4, quart, 2 * k)
        eids = me * ne + jnp.arange(ne)
        ys = []
        for i in range(CHUNKS):
            part = gi[:, :, i * run:(i + 1) * run].transpose(1, 0, 2, 3).reshape(-1, 2 * k)
            acc = expert_call(us[i], *plan(part[:, k:].astype(jnp.int32), part[:, :k], eids), w1, w3, w2, run)
            moe = lax.psum_scatter(acc, 'ep', scatter_dimension=0, tiled=True)
            moe = moe.reshape(4, run, d)
            ys.append((h4[:, i * run:(i + 1) * run].astype(jnp.float32) + moe).astype(jnp.bfloat16))
        y = jnp.concatenate(ys, axis=1)
        y = lax.all_to_all(y, 'replica', 0, 0, axis_index_groups=quads, tiled=True)
        return y.reshape(b, s, d)

    return jax.shard_map(local, mesh=mesh,
                         in_specs=(tok, rows_ep, rows_ep, rows_ep, rows_ep, P(None, None),
                                   by_expert, by_expert, by_expert, tok),
                         out_specs=tok, check_vma=False)
```

time: 7660 us -> 527 us (0.07); the launches traced: 7560 us -> 518 us
  blocking collectives: 5080 us -> 35 us
  local copies, waits for them, and re-layouts: 956 us -> 16.5 us
  other arithmetic: 736 us -> 18.7 us
  loops' own time: 389 us -> 0 us
  Pallas kernels: 0 us -> 245 us
  matrix products: 138 us -> 3.57 us
    all_to_all x1, blocking collectives: 5080 us -> 15.4 us  [local(): y = lax.all_to_all(y, 'replica', 0, 0, axis_index_groups=quads, tiled=True)]
    scatter-add x17 -> x0, other arithmetic: 635 us -> none  [the longest x15 355 us: work(): return acc.at[rb].add(gb[:, None] * o.astype(jnp.float32))]
    gather x32 -> x0, local copies, waits for them, and re-layouts: 568 us -> none  [the longest x1 186 us: expert_sum(): gate = jnp.where(ok, gates[jnp.minimum(cand, m - 1)], 0.0)]
    another operation x266 -> x0, loops' own time: 389 us -> none  [the longest x1 360 us: expert_sum(): lax.scan(body, jnp.zeros((n, d), jnp.float32), (jnp.arange(cand.shape[0])...]
    pallas_call x0 -> x3, Pallas kernels: none -> 245 us  [the longest x1 159 us: attention_call(): pl.pallas_call(functools.partial(attention_kernel, nr=nr, ne=ne), out_sha...]
    all_gather x4 -> x2, waiting for transfers between devices: 227 us -> 16.2 us  [local(): lax.all_gather(u4[:, i * run:(i + 1) * run].reshape(4 * run, d), 'ep', ax...]
    reduce_scatter x0 -> x2, waiting for transfers between devices: none -> 168 us  [local(): moe = lax.psum_scatter(acc, 'ep', scatter_dimension=0, tiled=True)]
    dynamic_slice x279 -> x0, local copies, waits for them, and re-layouts: 164 us -> none  [expert_sum(): lax.scan(body, jnp.zeros((n, d), jnp.float32), (jnp.arange(cand.shape[0])...]
  transfers between devices with their start and end apart: 7 -> 4, of which waited for: 4 -> 4; matrix products, arithmetic and copies ran while one was open for 13% -> 5% of each run, Pallas kernels for 0% -> 17%
where the time goes in v1:
time: 527 us; the launch traced here: 518 us
  Pallas kernels  245 us (46%)
  waiting for transfers between devices  185 us (35%)
  blocking collectives  35 us (7%)
  other arithmetic  18.7 us (4%)
  local copies, waits for them, and re-layouts  16.5 us (3%)
  between operations  13.9 us (3%)
    reduce_scatter x2, waiting for transfers between devices, local(): moe = lax.psum_scatter(acc, 'ep', scatter_dimension=0, tiled=True)  168 us
    pallas_call x1, Pallas kernels, attention_call(): pl.pallas_call(functools.partial(attention_kernel, nr=nr, ne=ne), out_sha...  159 us
    pallas_call x2, Pallas kernels, expert_call(): pl.pallas_call(functools.partial(expert_kernel, cap=cap, run=run), out_sh...  85.6 us
    all_gather x1, blocking collectives, local(): lax.all_gather(jnp.concatenate([g, ids.astype(jnp.float32)], axis=1), 'ep...  19.6 us
    all_gather x2, waiting for transfers between devices, local(): lax.all_gather(u4[:, i * run:(i + 1) * run].reshape(4 * run, d), 'ep', ax...  16.2 us
    all_to_all x1, blocking collectives, local(): y = lax.all_to_all(y, 'replica', 0, 0, axis_index_groups=quads, tiled=True)  15.4 us
  transfers between devices with their start and end apart: 4, of which 4 were waited for; matrix products, arithmetic and copies ran while one was open for 5% of the time, Pallas kernels for 17%

profile of v1, /device:TPU:21, one launch (start us, length us, event | category | flops | bytes accessed | tf_op | source)
XLA Modules:
  0.0 518.3 jit_solution(16924451019913255001)
XLA Ops:
  6.6 0.5 fusion.21
  7.1 0.8 copy.93
  7.9 0.7 pad.11.clone
  8.6 0.8 pad_maximum_fusion.1
  9.4 159.4 %attention.1 = (bf16[256,2048]{1,0:T(8,128)(2,1)}, s32[4,64,128]{2,1,0:T(8,128)}) custom-call(bf16[256,2048]{1,0:T(8,128)(2,1)} %bitcast.106, s32[4,64,128]{2,1,0:T(8,128)} %bitcast.94, bf16[128,4096]{1,0:T(8,128)(2,1)} %wq_hbm.1, bf16[128,4096]{1,0:T(8,128)(2,1)} %wk_hbm.1, bf16[128,4096]{1,0:T(8,128)(2,1)} %wv_hbm.1, bf16[256,2048]{1,0:T(8,128)(2,1)} %wo_hbm.1, ...), custom_call_target="tpu_custom_call" | custom-call | flops 99999997952 | bytes 30000000 | tf_op jit(solution)/shard_map/attention/pallas_call | solution.py:299
  168.8 1.5 fusion.2
  170.3 1.5 fusion
  171.8 1.2 fusion.26
  173.1 0.7 all-gather.4.cloned.1.call-update
  173.9 0.2 reduce-scatter.5.cloned.1.call-start
  174.1 1.0 copy.92
  175.1 3.2 fusion.1
  178.2 1.7 select_reduce_fusion.4
  180.2 19.6 %all-gather = f32[4096,16]{0,1:T(8,128)S(1)} all-gather(f32[256,16]{0,1:T(8,128)S(1)} %pad_maximum_fusion.3), channel_id=2, replica_groups=mesh['replica'=4,'ep'=16] {'ep'}, dimensions={0}, use_global_device_ids=true | all-gather | bytes 278528 | tf_op jit(solution)/shard_map/all_gather | solution.py:533
  199.8 0.3 reshape.156
  200.2 0.3 slice_bitcast_fusion
  200.6 0.2 reshape.162
  200.9 0.2 reshape.157
  201.2 0.2 compare_reduce_fusion.1
  201.4 0.2 reduce_sum.163
  201.9 0.2 reduce_sum.156
  202.6 0.3 copy.91
  203.2 0.2 fusion.6
  203.4 2.1 select_reduce_fusion
  205.4 0.6 copy.97
  206.3 4.1 select_reduce_fusion.3
  210.4 0.6 copy.96
  211.1 0.7 reshape.170.dense_ref
  211.7 1.0 pad.13.gate_ref
  212.8 0.7 convert_reduce_fusion.1.nsp_ref
  213.5 12.5 %all-gather.6.cloned.1.call-done.u_hbm = bf16[2048,2048]{1,0:T(8,128)(2,1)} async-done(((bf16[128,2048]{1,0:T(8,128)(2,1)}), bf16[2048,2048]{1,0:T(8,128)(2,1)}) %all-gather.6.cloned.1.call-update) | async-done | bytes 8388624 | tf_op jit(solution)/shard_map/all_gather | solution.py:532
  226.0 42.8 %experts.3 = f32[32768,128]{1,0:T(8,128)} custom-call(s32[8]{0:T(128)} %convert_reduce_fusion.1.nsp_ref, s32[64]{0:T(128)} %reshape.170.dense_ref, s32[2048]{0:T(1024)} %bitcast.104, f32[2048]{0:T(1024)} %bitcast.102, f32[2048,128]{1,0:T(8,128)} %pad.13.gate_ref, bf16[2048,2048]{1,0:T(8,128)(2,1)} %all-gather.6.cloned.1.call-done.u_hbm, ...), custom_call_target="tpu_custom_call" | custom-call | flops 60000002048 | bytes 160000000 | tf_op jit(solution)/shard_map/experts/pallas_call | solution.py:465
  268.9 0.3 copy.87
  269.3 1.0 pad.12.gate_ref
  270.3 2.0 select_reduce_fusion.2
  272.4 0.6 copy.95
  273.0 0.6 copy.94
  273.6 0.6 reshape.168.dense_ref
  274.2 0.7 convert_reduce_fusion.3.nsp_ref
  274.9 3.7 all-gather.4.cloned.1.call-done.u_hbm
  278.6 42.8 %experts.2 = f32[32768,128]{1,0:T(8,128)} custom-call(s32[8]{0:T(128)} %convert_reduce_fusion.3.nsp_ref, s32[64]{0:T(128)} %reshape.168.dense_ref, s32[2048]{0:T(1024)} %bitcast.105, f32[2048]{0:T(1024)} %bitcast.103, f32[2048,128]{1,0:T(8,128)} %pad.12.gate_ref, bf16[2048,2048]{1,0:T(8,128)(2,1)} %all-gather.4.cloned.1.call-done.u_hbm, ...), custom_call_target="tpu_custom_call" | custom-call | flops 60000002048 | bytes 160000000 | tf_op jit(solution)/shard_map/experts/pallas_call | solution.py:465
  321.5 71.4 %reduce-scatter.5.cloned.1.call-done = f32[2048,128]{1,0:T(8,128)} async-done(((f32[32768,128]{1,0:T(8,128)}), f32[2048,128]{1,0:T(8,128)}) %reduce-scatter.5.cloned.1.call-update) | async-done | bytes 1048592 | tf_op jit(solution)/shard_map/reduce_scatter | solution.py:540
  392.9 1.4 reshape.165
  394.3 96.8 %reduce-scatter.3.cloned.1.call-done = f32[2048,128]{1,0:T(8,128)} async-done(((f32[32768,128]{1,0:T(8,128)}), f32[2048,128]{1,0:T(8,128)}) %reduce-scatter.3.cloned.1.call-update) | async-done | bytes 1048592 | tf_op jit(solution)/shard_map/reduce_scatter | solution.py:540
  491.1 2.4 reshape.161
  493.4 1.5 add_convert_fusion.1
  495.0 15.4 %all_to_all.5 = bf16[4,64,2048]{2,1,0:T(8,128)(2,1)S(1)} all-to-all(bf16[4,64,2048]{2,1,0:T(8,128)(2,1)S(1)} %pad_maximum_fusion), channel_id=1, replica_groups={{0,16,32,48},{1,17,33,49},{2,18,34,50},{3,19,35,51},{4,20,36,52},{5,21,..., dimensions={0} | all-to-all | bytes 2097152 | tf_op jit(solution)/shard_map/all_to_all | solution.py:544
  510.4 1.0 copy.99
  (51 shorter events, 2.1 us)
Async XLA Ops:
  6.5 168.5 %copy-start = (f32[2048,128]{1,0:T(8,128)S(1)}, f32[2048,128]{1,0:T(8,128)}, u32[]{:S(2)}) copy-start(f32[2048,128]{1,0:T(8,128)} %param.15) | copy-start | bytes 3145732
  6.6 219.4 %all-gather.6.cloned.1.call-start = ((), (), s32[]{:S(2)}) async-start(), calls=%async_computation.5 | async-start | bytes 8912896 | tf_op jit(solution)/shard_map/all_gather | solution.py:532
  173.1 105.6 %all-gather.4.cloned.1.call-start = ((), (), s32[]{:S(2)}) async-start(), calls=%async_computation.3 | async-start | bytes 8912896 | tf_op jit(solution)/shard_map/all_gather | solution.py:532
  173.9 219.0 %reduce-scatter.5.cloned.1.call-start = ((), (), s32[]{:S(2)}) async-start(), calls=%async_computation.6 | async-start | bytes 17825792 | tf_op jit(solution)/shard_map/reduce_scatter | solution.py:540
  268.9 222.2 %reduce-scatter.3.cloned.1.call-start = ((), (), s32[]{:S(2)}) async-start(), calls=%async_computation.4 | async-start | bytes 17825792 | tf_op jit(solution)/shard_map/reduce_scatter | solution.py:540
  278.6 232.7 %copy-start.1 = (f32[2048,128]{1,0:T(8,128)S(1)}, f32[2048,128]{1,0:T(8,128)}, u32[]{:S(2)}) copy-start(f32[2048,128]{1,0:T(8,128)} %param.15) | copy-start | bytes 3145732
  321.4 172.0 %copy-start.2 = (bf16[256,2048]{1,0:T(8,128)(2,1)S(1)}, bf16[256,2048]{1,0:T(8,128)(2,1)}, u32[]{:S(2)}) copy-start(bf16[256,2048]{1,0:T(8,128)(2,1)} %get-tuple-element.7) | copy-start | bytes 3145732
Sparse Core Ops, SparseCore 0:
  173.2 52.7 all-gather.5
  227.6 50.9 all-gather.3
  281.0 111.8 reduce-scatter.4
  395.1 95.9 reduce-scatter.2

commit v2 on v0

v2 whole, which is shorter than its diff:
```python
import functools
import math
import types
import jax
import jax.numpy as jnp
import numpy as np
from jax import lax
from jax.experimental import pallas as pl
from jax.experimental.pallas import tpu as pltpu
from jax.sharding import PartitionSpec as P

HEAD = 128
EPS = 1e-6
THETA = 10000.0
SPM = 128
DENSE_AT = 32
LANES = 128
FU = 2
RUNS = (32, 32)


WAYS = range(2)
QUAD = range(4)


def lanes(j):
    return slice(j * LANES, (j + 1) * LANES)


def octet(i):
    return pl.ds(8 * i, 8)


def remote(src, dst, ssem, rsem, rep, ep):
    return pltpu.make_async_remote_copy(src_ref=src, dst_ref=dst, send_sem=ssem, recv_sem=rsem,
                                        device_id={'replica': rep, 'ep': ep}, device_id_type=pl.DeviceIdType.MESH)


def meet(peers):
    barrier = pltpu.get_barrier_semaphore()
    for rep, ep in peers:
        pl.semaphore_signal(barrier, device_id={'replica': rep, 'ep': ep}, device_id_type=pl.DeviceIdType.MESH)
    pl.semaphore_wait(barrier, len(peers))


def place(nr, ne):
    side, nz = math.isqrt(nr), ne // 2
    r, e = lax.axis_index('replica'), lax.axis_index('ep')
    z, c = e // 2, e % 2
    px, py = r // side, r % side
    qx, qy = px % 2, py % 2
    nx, ny = 1 - qx, 1 - qy

    def quad(x, y):
        return (px - qx + x) * side + py - qy + y

    return types.SimpleNamespace(
        r=r, e=e, z=z, c=c, q=2 * qx + qy, par=(qx + qy) % 2, far=nz // 2, nz=nz, mate=e + 1 - 2 * c,
        beside=(quad(nx, qy), quad(qx, ny), quad(nx, ny)), seqs=(2 * nx + qy, 2 * qx + ny, 2 * nx + ny),
        ring=((e + 2) % ne, (e + ne - 2) % ne), quad=lambda j: quad(j // 2, j % 2),
        step=lambda way, dist: (z + (nz - dist if way else dist)) % nz)


def rmsnorm(v):
    v = v.astype(jnp.float32)
    return v * lax.rsqrt(jnp.mean(v * v, axis=-1, keepdims=True) + EPS)


ALONG = (1, 2, 3, 5, 6, 7)
BESIDE = (6, 7)


def attention_kernel(x_hbm, idx_hbm, wq_hbm, wk_hbm, wv_hbm, wo_hbm, cos_ref, sin_ref, h_ref, idx_ref, *rest, nr, ne, runs):
    u_refs = rest[:len(runs)]
    (xall, wqkv, stage, wov, obuf, orecv, acc, lsem, xs_s, xs_r, ix_s, ix_r, wd_s, wd_r, od_r, oo_r,
     wa_s, wa_r, wb_s, wb_r, oz_s, oz_r, oxy_s, oxy_r, od_s, oo_s) = rest[len(runs):]
    me = place(nr, ne)
    r, e, z, c, q, par, far, nz, mate, ring = me.r, me.e, me.z, me.c, me.q, me.par, me.far, me.nz, me.mate, me.ring
    events = 3 * far - 1
    s, d = x_hbm.shape
    wrows, cols = wqkv.shape[1] // ne, wqkv.shape[2]
    orows = wov.shape[1] // 2
    quart = s // 4
    unit = orows // 16
    mine = 2 * q + c

    def came(way, dist):
        return me.step(1 - way, dist)

    def al(v, m):
        return pl.multiple_of(v, m)

    loads = [pltpu.make_async_copy(x_hbm, xall.at[mine], lsem.at[0])]
    for w, ref in enumerate((wq_hbm, wk_hbm, wv_hbm)):
        loads.append(pltpu.make_async_copy(ref.at[:, pl.ds(al(mine * cols, cols), cols)],
                                           wqkv.at[w, pl.ds(al(e * wrows, wrows), wrows)], lsem.at[1 + w]))
        loads.append(pltpu.make_async_copy(ref.at[:, pl.ds(al((2 * q + 1 - c) * cols, cols), cols)],
                                           stage.at[w, z], lsem.at[4 + w]))
    loads.append(pltpu.make_async_copy(wo_hbm, wov.at[z, pl.ds(al(c * orows, orows), orows)], lsem.at[7]))
    loads.append(pltpu.make_async_copy(idx_hbm, idx_ref.at[q], lsem.at[8]))
    for cp in loads:
        cp.start()

    meet([(rep, ep) for rep in me.beside for ep in (e, mate)] + [(r, mate), (r, ring[0]), (r, ring[1])])
    for cp in loads:
        cp.wait()

    sent = []

    def go(make, *key):
        make(*key).start()
        sent.append((make, key))

    def part_a(zz):
        return wqkv.at[:, pl.ds(al((2 * zz + c) * wrows, wrows), wrows)]

    def part_b(zz):
        return stage.at[:, zz]

    def ring_a(way, dist, hop=1):
        at = part_a(came(way, dist - hop))
        return remote(at, at, wa_s.at[way, dist - 1], wa_r.at[way, dist - 1], r, ring[way])

    def ring_b(way, dist, hop=1):
        at = part_b(came(way, dist - hop))
        return remote(at, at, wb_s.at[way, dist - 1], wb_r.at[way, dist - 1], r, ring[way])

    def cross_w(way, dist):
        zz = came(way, dist)
        k = dist if way == 0 else nz - dist
        return remote(part_b(zz), part_a(zz), wd_s.at[k], wd_r.at[zz], r, mate)

    def x_to(k):
        at = xall.at[mine]
        return remote(at, at, xs_s.at[k], xs_r.at[mine], (*me.beside, r)[k], mate if k == len(me.beside) else e)

    def x_on(k):
        at = xall.at[2 * me.seqs[k] + c]
        return remote(at, at, xs_s.at[4 + k], xs_r.at[2 * me.seqs[k] + c], r, mate)

    def idx_to(k):
        return remote(idx_hbm, idx_ref.at[q], ix_s.at[k], ix_r.at[q], me.beside[k], e)

    def order(way, i):
        return (1 + i // 3, i % 3) if i < events - 2 else (far, way if i == events - 2 else 2)

    def rows_o(zz, dist, kind, p, way):
        if kind < 2:
            first, n = (16 - 2 * FU) * unit * p + FU * unit * kind, FU * unit
        elif dist < far:
            first, n = 2 * FU * unit, (16 - 4 * FU) * unit
        else:
            first, n = (2 * FU + (8 - 2 * FU) * way) * unit, (8 - 2 * FU) * unit
        return wov.at[zz, pl.ds(al(c * orows + first, unit), n)]

    def ring_o(way, i, hop=1):
        dist, kind = order(way, i)
        at = rows_o(came(way, dist - hop), dist, kind, par, way)
        return remote(at, at, oz_s.at[way, i], oz_r.at[way, i], r, ring[way])

    def side_o(way, i, p=par):
        dist, kind = order(way, i)
        at = rows_o(came(way, dist), dist, kind, p, way)
        return remote(at, at, oxy_s.at[way, i], oxy_r.at[way, i], me.beside[kind], e)

    def cross_o(way, i, other):
        dist, kind = order(way, i)
        zz = came(way, dist)
        at = rows_o(zz, dist, kind, 1 - par if other else par, way)
        return remote(at, at, od_s.at[2 * other + way, i], od_r.at[zz], r, mate)

    def own_o():
        at = wov.at[z, pl.ds(al(c * orows, orows), orows)]
        return remote(at, at, od_s.at[4, 0], od_r.at[z], r, mate)

    for way in WAYS:
        go(ring_a, way, 1)
    for way in WAYS:
        go(ring_b, way, 1)
    go(cross_w, 0, 0)
    for k in QUAD:
        go(x_to, k)
    for k in range(len(me.beside)):
        go(idx_to, k)

    def wait_w(dist):
        for way in WAYS:
            if dist <= far - way:
                ring_a(way, dist, 0).wait_recv()
                if dist + 1 <= far - way:
                    go(ring_a, way, dist + 1)
        for way in WAYS:
            if dist <= far - 1 + way:
                ring_b(way, dist, 0).wait_recv()
                if dist + 1 <= far - 1 + way:
                    go(ring_b, way, dist + 1)
                go(cross_w, way, dist)

    def pass_x(k):
        x_on(k).wait_recv()
        go(x_on, k)

    def serve(i):
        for way in WAYS:
            dist, kind = order(way, i)
            ring_o(way, i, 0).wait_recv()
            if dist + 1 < far:
                go(ring_o, way, i + 3)
            elif dist < far and kind in (way, 2):
                go(ring_o, way, events - 2 + (kind == 2))
            if kind < 2:
                go(side_o, way, i)
            go(cross_o, way, i, 0)

    def serve_side(i):
        for way in WAYS:
            side_o(way, i, 1 - par).wait_recv()
            go(cross_o, way, i, 1)

    for dist in range(1, far):
        wait_w(dist)
        if dist == max(1, far - 2):
            pass_x(0)
            pass_x(1)
    for i in range(3):
        for way in WAYS:
            go(ring_o, way, i)
    go(own_o)
    pass_x(2)
    wait_w(far)
    for zz in range(nz):
        at = wqkv.at[:, pl.ds((2 * zz + 1 - c) * wrows, wrows)]
        remote(at, at, wd_s.at[0], wd_r.at[zz], r, mate).wait_recv()
    for j in QUAD:
        at = xall.at[2 * j + 1 - c]
        remote(at, at, xs_s.at[0], xs_r.at[2 * j + 1 - c], r, mate).wait_recv()

    nh = cols // HEAD
    scale = 1.0 / math.sqrt(HEAD)

    def o_to(t, k):
        return remote(obuf.at[t, pl.ds(quart * k, quart)], orecv.at[mine, pl.ds(al(quart * (t // 2), quart), quart)],
                      oo_s.at[t, k], oo_r.at[mine], me.quad(k), 2 * z + t % 2)

    def send_o(t):
        for k in QUAD:
            @pl.when((q != k) | (c != t % 2))
            def _():
                o_to(t, k).start()

            @pl.when((q == k) & (c == t % 2))
            def _():
                orecv[mine, pl.ds(al(quart * (t // 2), quart), quart), :] = obuf[t, pl.ds(quart * k, quart), :]

    def sequence(t, carry):
        a = rmsnorm(xall[t]).astype(jnp.bfloat16)
        qf, kf, vf = [jnp.dot(a, wqkv[w], preferred_element_type=jnp.float32) for w in range(wqkv.shape[0])]
        cs, sn = cos_ref[...], sin_ref[...]
        row = lax.broadcasted_iota(jnp.int32, (s, s), 0)
        col = lax.broadcasted_iota(jnp.int32, (s, s), 1)
        for n in range(nh):
            at = slice(n * HEAD, (n + 1) * HEAD)
            qh, kh = qf[:, at], kf[:, at]
            qh = (qh * cs + pltpu.roll(qh, HEAD // 2, 1) * sn).astype(jnp.bfloat16)
            kh = (kh * cs + pltpu.roll(kh, HEAD // 2, 1) * sn).astype(jnp.bfloat16)
            sc = lax.dot_general(qh, kh, (((1,), (1,)), ((), ())), preferred_element_type=jnp.float32) * scale
            sc = jnp.where(row >= col, sc, -1e30)
            p = jnp.exp(sc - jnp.max(sc, axis=-1, keepdims=True))
            p = (p * (1.0 / jnp.sum(p, axis=-1, keepdims=True))).astype(jnp.bfloat16)
            obuf[t, :, at] = jnp.dot(p, vf[:, at].astype(jnp.bfloat16), preferred_element_type=jnp.float32).astype(jnp.bfloat16)

        @pl.when(t > 0)
        def _():
            send_o(t - 1)
        for i, n in enumerate(ALONG):
            @pl.when(t == n)
            def _():
                serve(i)
        for i, n in enumerate(BESIDE):
            @pl.when(t == n)
            def _():
                serve_side(i)
        return carry

    lax.fori_loop(0, nz, sequence, 0)
    send_o(nz - 1)
    serve_side(3)
    serve(6)
    serve_side(4)
    serve(7)

    for k in range(nz):
        @pl.when(k != mine)
        def _():
            at = orecv.at[k]
            remote(at, at, oo_s.at[0, 0], oo_r.at[k], r, mate).wait_recv()

    for j in QUAD:
        acc[pl.ds(quart * j, quart), :] = xall[2 * j + c, pl.ds(al(quart * q, quart), quart), :].astype(jnp.float32)

    def project(way, dist):
        zz = came(way, dist)
        at = wov.at[zz, pl.ds(al((1 - c) * orows, orows), orows)]
        remote(at, at, od_s.at[0, 0], od_r.at[zz], r, mate).wait_recv()
        width = min(512, d)

        def chunk(n, carry):
            cut = pl.ds(al(n * width, width), width)
            acc[:, cut] = acc[:, cut] + jnp.dot(orecv[zz], wov[zz, :, cut], preferred_element_type=jnp.float32)
            return carry

        lax.fori_loop(0, d // width, chunk, 0)

    def both(dist):
        for way in WAYS:
            project(way, dist)

    project(0, 0)
    both(1)
    serve(8)
    serve_side(6)
    serve_side(7)
    both(2)
    serve(9)
    serve(10)
    both(3)
    serve_side(9)
    project(0, far)
    h_ref[...] = acc[...].astype(jnp.bfloat16)
    acc[...] = rmsnorm(h_ref[...])
    first = 0
    for run, u_ref in zip(runs, u_refs):
        for j in QUAD:
            u_ref[run * j:run * (j + 1), :] = acc[quart * j + first:quart * j + first + run, :].astype(jnp.bfloat16)
        first += run
    for k in range(len(me.beside)):
        at = idx_ref.at[me.seqs[k]]
        remote(idx_hbm, at, ix_s.at[k], ix_r.at[me.seqs[k]], me.beside[k], e).wait_recv()
    for t in range(nz):
        for k in QUAD:
            @pl.when((q != k) | (c != t % 2))
            def _():
                o_to(t, k).wait_send()
    for make, key in sent:
        make(*key).wait_send()


def attention_call(x, idx, wq, wk, wv, wo, nr, ne, runs):
    s, d = x.shape
    nz = ne // 2
    events = 3 * (nz // 2) - 1
    half = HEAD // 2
    freq = THETA ** (-np.arange(half, dtype=np.float32) / half)
    ang = np.arange(s, dtype=np.float32)[:, None] * freq.astype(np.float32)
    cos, sin = np.cos(ang), np.sin(ang)
    cos = np.concatenate([cos, cos], axis=1)
    sin = np.concatenate([-sin, sin], axis=1)
    any_ = pl.BlockSpec(memory_space=pl.ANY)
    vmem = pl.BlockSpec(memory_space=pltpu.VMEM)
    bf = jnp.bfloat16
    dma = pltpu.SemaphoreType.DMA
    heads = pltpu.VMEM((nz, s, wq.shape[1] // nz), bf)
    h, ids, *us = pl.pallas_call(
        functools.partial(attention_kernel, nr=nr, ne=ne, runs=runs),
        out_shape=(jax.ShapeDtypeStruct((s, d), bf), jax.ShapeDtypeStruct((len(QUAD),) + idx.shape, idx.dtype),
                   *[jax.ShapeDtypeStruct((len(QUAD) * run, d), bf) for run in runs]),
        in_specs=[any_, any_, any_, any_, any_, any_, vmem, vmem],
        out_specs=(vmem, vmem, *[vmem for _ in runs]),
        scratch_shapes=[
            pltpu.VMEM((nz, s, d), bf),
            pltpu.VMEM((3, d, wq.shape[1] // nz), bf),
            pltpu.VMEM((3, nz, d // ne, wq.shape[1] // nz), bf),
            pltpu.VMEM((nz, 2 * wo.shape[0], d), bf),
            heads, heads,
            pltpu.VMEM((s, d), jnp.float32),
            dma((9,)), *[dma((nz,))] * 8, *[dma((2, events))] * 8, dma((5, events)), dma((nz, len(QUAD))),
        ],
        compiler_params=pltpu.CompilerParams(collective_id=0, has_side_effects=True, vmem_limit_bytes=60 * 2**20),
        cost_estimate=pl.CostEstimate(flops=100 * 10**9, bytes_accessed=30 * 10**6, transcendentals=10**6),
        name='attention',
    )(x, idx, wq, wk, wv, wo, jnp.asarray(cos), jnp.asarray(sin))
    return h, us, ids


def expert_kernel(nsp_ref, dense_ref, list_ref, glist_ref, gate_ref, u_hbm, w1, w3, w2, out_hbm,
                  uw, acc, ubuf, wup, wdown, act, xs, zs, up_sem, down_sem, in_sem, out_sem, *, cap, run):
    ne, d, f = w1.shape
    t = u_hbm.shape[0]
    ndev = t // (4 * run)
    per = ndev // 2
    blk = per * run
    nb = t // blk
    seg = d // LANES
    eight = 8 * seg
    wide = 4 * LANES

    def tile(g, j):
        return pl.ds(g * eight + 8 * j, 8)

    def fetch_up(slot, e):
        for k, w in enumerate((w1, w3)):
            pltpu.make_async_copy(w.at[e], wup.at[slot, k], up_sem.at[slot, k]).start()

    nd = wdown.shape[0]

    def fetch_down(e):
        e = jnp.asarray(e, jnp.int32)
        pltpu.make_async_copy(w2.at[e], wdown.at[e % nd], down_sem.at[e % nd]).start()

    def load(b):
        b = jnp.asarray(b, jnp.int32)
        j, first = b // (nb // 4), (b % (nb // 4)) * per
        for k in range(per):
            src = u_hbm.at[pl.ds(pl.multiple_of(((first + k) * 4 + j) * run, run), run)]
            pltpu.make_async_copy(src, ubuf.at[b % 2, pl.ds(k * run, run)], in_sem.at[b % 2]).start()

    load(0)
    load(1)
    fetch_up(0, 0)
    fetch_down(0)

    def clear(i, carry):
        acc[pl.ds(pl.multiple_of(i * eight, eight), eight), :] = jnp.zeros((eight, LANES), jnp.float32)
        return carry

    lax.fori_loop(0, t // 8 + 1, clear, 0)
    uw[pl.ds(t * seg, eight), :] = jnp.zeros((eight, LANES), jnp.float32)

    def widen(b, carry):
        at = ubuf.at[b % 2]
        pltpu.make_async_copy(at, at, in_sem.at[b % 2]).wait()
        to = uw.at[pl.ds(pl.multiple_of(b * blk * seg, eight), blk * seg)]
        for g in range(0, blk // 8, 2):
            for j in range(seg):
                for n, v in enumerate(jnp.split(at[8 * g:8 * g + 16, lanes(j)].astype(jnp.float32), 2)):
                    to[tile(g + n, j), :] = v

        @pl.when(b + 2 < nb)
        def _():
            load(b + 2)
        return carry

    lax.fori_loop(0, nb, widen, 0)
    x = ubuf.at[0]

    def narrow(src, rows):
        for g in range(0, rows // 8, 2):
            for j in range(seg):
                pair = [src[tile(g + n, j), :] for n in WAYS]
                x[8 * g:8 * g + 16, lanes(j)] = jnp.concatenate(pair).astype(jnp.bfloat16)

    def hidden(slot, rows):
        for c in range(0, f, 256):
            a1 = jnp.dot(x[:rows, :], wup[slot, 0, :, c:c + 256], preferred_element_type=jnp.float32)
            a3 = jnp.dot(x[:rows, :], wup[slot, 1, :, c:c + 256], preferred_element_type=jnp.float32)
            act[:rows, c:c + 256] = (jax.nn.silu(a1) * a3).astype(jnp.bfloat16)

    def expert(e, carry):
        slot = lax.rem(e, 2)

        @pl.when(e + 1 < ne)
        def _():
            fetch_up(1 - slot, e + 1)
            if nd == 2:
                fetch_down(e + 1)

        for j in WAYS:
            pltpu.make_async_copy(wup.at[slot, j], wup.at[slot, j], up_sem.at[slot, j]).wait()
        down = wdown.at[e % nd]
        pltpu.make_async_copy(down, down, down_sem.at[e % nd]).wait()

        def block(b, carry):
            @pl.when(dense_ref[e * nb + b] != 0)
            def _():
                part = pl.ds(pl.multiple_of(b * blk * seg, eight), blk * seg)
                narrow(uw.at[part], blk)
                hidden(slot, blk)
                g8 = gate_ref[b].T[:blk]
                lane = lax.broadcasted_iota(jnp.int32, g8.shape, 1)
                gate = jnp.sum(jnp.where(lane == e, g8, 0.0), axis=1, keepdims=True)
                to = acc.at[part]
                for c in range(0, d, wide):
                    z = jnp.dot(act[:blk, :], down[:, c:c + wide], preferred_element_type=jnp.float32)
                    z = z.astype(jnp.bfloat16).astype(jnp.float32)
                    z = jnp.where(gate != 0.0, gate * z, 0.0)
                    for g in range(blk // 8):
                        for j in range(wide // LANES):
                            at = tile(g, c // LANES + j)
                            to[at, :] = to[at, :] + z[8 * g:8 * g + 8, lanes(j)]
            return carry

        lax.fori_loop(0, nb, block, 0)
        n = nsp_ref[e]

        def gathered(i, carry):
            base = e * cap + i * SPM
            groups = (jnp.minimum(n - i * SPM, SPM) + 7) // 8

            def token(first):
                return pl.ds(first, seg, stride=8)

            def gather(q, carry):
                for s in range(8):
                    xs[token(q * eight + s), :] = uw[token(list_ref[base + q * 8 + s]), :]
                return carry

            lax.fori_loop(0, groups, gather, 0)
            narrow(xs, SPM)
            hidden(slot, SPM)
            for c in range(0, d, wide):
                z = jnp.dot(act[:SPM, :], down[:, c:c + wide], preferred_element_type=jnp.float32)
                z = z.astype(jnp.bfloat16).astype(jnp.float32)
                for g in range(SPM // 8):
                    for j in range(wide // LANES):
                        zs[tile(g, c // LANES + j), :] = z[8 * g:8 * g + 8, lanes(j)]

            def scatter(q, carry):
                for s in range(8):
                    i = base + q * 8 + s
                    at = token(list_ref[i])
                    acc[at, :] = acc[at, :] + glist_ref[i] * zs[token(q * eight + s), :]
                return carry

            lax.fori_loop(0, groups, scatter, 0)
            return carry

        lax.fori_loop(0, (n + SPM - 1) // SPM, gathered, 0)

        if nd == 1:
            @pl.when(e + 1 < ne)
            def _():
                fetch_down(e + 1)
        return carry

    lax.fori_loop(0, ne, expert, 0)

    def store(k, carry):
        for j in QUAD:
            src = acc.at[pl.ds(pl.multiple_of((j * ndev + k) * run * seg, run * seg), run * seg)]
            dst = out_hbm.at[pl.ds(pl.multiple_of((k * 4 + j) * run * seg, run * seg), run * seg)]
            pltpu.make_async_copy(src, dst, out_sem).start()
        return carry

    lax.fori_loop(0, ndev, store, 0)
    pltpu.make_async_copy(acc.at[pl.ds(0, t * seg)], out_hbm, out_sem).wait()


def expert_call(u, gates, nsp, dense, rows, glist, w1, w3, w2, run):
    t, d = u.shape
    ne, _, f = w1.shape
    cap = rows.shape[0] // ne
    seg = d // LANES
    blk = t // 8
    dma = pltpu.SemaphoreType.DMA

    def rows_of(n):
        return pltpu.VMEM((n * seg, LANES), jnp.float32)

    any_ = pl.BlockSpec(memory_space=pl.ANY)
    smem = pl.BlockSpec(memory_space=pltpu.SMEM)
    return pl.pallas_call(
        functools.partial(expert_kernel, cap=cap, run=run),
        out_shape=jax.ShapeDtypeStruct((t * seg, LANES), jnp.float32),
        in_specs=[smem] * 4 + [pl.BlockSpec(memory_space=pltpu.VMEM)] + [any_] * 4,
        out_specs=any_,
        scratch_shapes=[
            rows_of(t + 8), rows_of(t + 8),
            pltpu.VMEM((2, max(blk, SPM), d), jnp.bfloat16),
            pltpu.VMEM((2, 2, d, f), jnp.bfloat16),
            pltpu.VMEM((2 if t <= 2048 else 1, f, d), jnp.bfloat16),
            pltpu.VMEM((max(blk, SPM), f), jnp.bfloat16),
            rows_of(SPM), rows_of(SPM),
            dma((2, 2)), dma((2,)), dma((2,)), dma(()),
        ],
        compiler_params=pltpu.CompilerParams(vmem_limit_bytes=63 * 2**20),
        cost_estimate=pl.CostEstimate(flops=60 * 10**9, bytes_accessed=160 * 10**6, transcendentals=10**6),
        name='experts',
    )(nsp, dense, rows, glist, gates, u, w1, w3, w2)


def plan(ids, g, eids, d):
    t = ids.shape[0]
    ne = eids.shape[0]
    nb = 8
    blk = t // nb
    cap = nb * DENSE_AT
    seg = d // LANES
    eq = ids[:, :, None] == eids
    gates = jnp.sum(jnp.where(eq, g[:, :, None], 0.0), axis=1)
    m = jnp.any(eq, axis=1)
    dense = jnp.sum(m.reshape(nb, blk, ne), axis=1, dtype=jnp.int32) >= DENSE_AT
    sp = m & ~jnp.repeat(dense, blk, axis=0)
    spb = sp.astype(jnp.bfloat16).reshape(-1, LANES, ne)

    def ahead(n):
        i = jnp.arange(n)
        return (i < i[:, None]).astype(jnp.bfloat16)

    inner = jnp.einsum('ij,bje->bie', ahead(LANES), spb, preferred_element_type=jnp.float32)
    outer = jnp.einsum('ij,jke->ie', ahead(t // LANES), spb, preferred_element_type=jnp.float32)
    pos = jnp.where(sp, (inner + outer[:, None]).reshape(t, ne).astype(jnp.int32), -1)
    nsp = jnp.sum(sp, axis=0, dtype=jnp.int32)
    at = pos.T[:, None] == jnp.arange(cap)[:, None]
    tok = jnp.arange(t)
    start = (tok // 8) * (8 * seg) + tok % 8 - t * seg
    rows = jnp.sum(jnp.where(at, start, 0), axis=-1, dtype=jnp.int32) + t * seg
    glist = jnp.sum(jnp.where(at, gates.T[:, None], 0.0), axis=-1)
    gates = jnp.pad(gates.reshape(nb, blk, ne).transpose(0, 2, 1), ((0, 0), (0, 0), (0, -blk % LANES)))
    return gates, nsp, dense.T.reshape(-1).astype(jnp.int32), rows.reshape(-1), glist.reshape(-1)


def combine_kernel(acc_hbm, moe_ref, h_ref, y_ref, own, other, passed, ybuf, lsem, cs_s, cs_r, rs_s, rs_r, ys_s, ys_r,
                   *, nr, ne, runs):
    me = place(nr, ne)
    r, e, z, c, q, far, nz, mate, ring, to = me.r, me.e, me.z, me.c, me.q, me.far, me.nz, me.mate, me.ring, me.step
    quart = y_ref.shape[0] // 4
    seg = y_ref.shape[1] // LANES
    eight = 8 * seg
    rows = own.shape[1]
    half = rows // 2

    def block(ep):
        return acc_hbm.at[pl.ds(pl.multiple_of(ep * rows, rows), rows)]

    near = [(0, far)] + [(way, dist) for dist in range(far - 1, 0, -1) for way in WAYS] + [(0, 0)]

    def load(k):
        zz = to(*near[k])
        return pltpu.make_async_copy(block(2 * zz + c), own.at[zz], lsem.at[k])

    def cross(k):
        zz = to(*near[k])
        return remote(block(2 * zz + 1 - c), other.at[zz], cs_s.at[k], cs_r.at[k], r, mate)

    def cut(h):
        return pl.ds(h * half, half)

    def source(way, dist, h):
        first = dist == far or (dist == far - 1 and h != way)
        return own.at[to(way, dist), cut(h)] if first else passed.at[way, dist, cut(h)]

    def hop(way, dist, h):
        return remote(source(way, dist, h), passed.at[way, dist - 1, cut(h)], rs_s.at[way, dist, h], rs_r.at[way, dist - 1, h],
                      r, ring[way])

    def came(way, dist, h):
        at = passed.at[way, dist, cut(h)]
        return remote(at, at, rs_s.at[way, dist, h], rs_r.at[way, dist, h], r, ring[way])

    def y_to(n, j):
        return remote(ybuf.at[j, pl.ds(sum(runs[:n]), runs[n])], y_ref.at[pl.ds(pl.multiple_of(quart * q + sum(runs[:n]), 8), runs[n])],
                      ys_s.at[n, j], ys_r.at[n, q], me.quad(j), e)

    def y_from(n, j):
        at = y_ref.at[pl.ds(quart * j + sum(runs[:n]), runs[n])]
        return remote(at, at, ys_s.at[n, j], ys_r.at[n, j], me.beside[0], e)

    for k in range(nz):
        load(k).start()
    meet([(rep, e) for rep in me.beside] + [(r, mate), (r, ring[0]), (r, ring[1])])
    for k in range(nz):
        cross(k).start()

    def give(n, j):
        @pl.when(q != j)
        def _():
            y_to(n, j).start()

        @pl.when(q == j)
        def _():
            y_ref[pl.ds(pl.multiple_of(quart * q + sum(runs[:n]), 8), runs[n]), :] = ybuf[j, sum(runs[:n]):sum(runs[:n + 1]), :]

    def finish(n, j, moe):
        first = sum(runs[:n])
        for i in range(runs[n] // 8):
            part = moe(i)
            for m in range(seg):
                at = slice(m * LANES, (m + 1) * LANES)
                hf = h_ref[quart * j + first + 8 * i:quart * j + first + 8 * i + 8, at].astype(jnp.float32)
                ybuf[j, first + 8 * i:first + 8 * i + 8, at] = (hf + part[8 * m:8 * m + 8]).astype(jnp.bfloat16)

    done = 0
    for n in range(len(runs) - 1):
        for j in QUAD:
            at = done + runs[n] * j
            finish(n, j, lambda i, at=at: moe_ref[(at // 8 + i) * eight:(at // 8 + i + 1) * eight, :])
        for j in QUAD:
            give(n, j)
        done += 4 * runs[n]

    def ready(k):
        load(k).wait()
        cross(k).wait_recv()
        zz = to(*near[k])

        def add(i, carry):
            at = pl.ds(pl.multiple_of(i * eight, eight), eight)
            own[zz, at, :] = own[zz, at, :] + other[zz, at, :]
            return carry

        lax.fori_loop(0, rows // eight, add, 0)

    def join(way, dist, h):
        came(way, dist, h).wait_recv()
        zz = to(way, dist)

        def add(i, carry):
            at = pl.ds(pl.multiple_of(h * half + i * eight, eight), eight)
            passed[way, dist, at, :] = passed[way, dist, at, :] + own[zz, at, :]
            return carry

        lax.fori_loop(0, half // eight, add, 0)

    ready(0)
    for way in WAYS:
        hop(way, far, way).start()
    k = 1
    for dist in range(far - 1, 0, -1):
        for way in WAYS:
            ready(k)
            k += 1
            if dist == far - 1:
                hop(way, dist, 1 - way).start()
        for late in WAYS:
            for way in WAYS:
                h = way if late else 1 - way
                if dist == far - 1 and not late:
                    continue
                join(way, dist, h)
                hop(way, dist, h).start()
    ready(k)
    last = len(runs) - 1
    for h in WAYS:
        join(0, 0, h)
    for h in WAYS:
        came(1, 0, h).wait_recv()
    per = runs[last] // 8
    for j in QUAD:
        def moe(i, j=j):
            at = slice((j * per + i) * eight, (j * per + i + 1) * eight)
            return passed[0, 0, at, :] + passed[1, 0, at, :]

        finish(last, j, moe)
    for j in QUAD:
        give(last, j)
    for n in range(len(runs)):
        for j in QUAD:
            @pl.when(q != j)
            def _():
                y_from(n, j).wait_recv()
                y_to(n, j).wait_send()
    for k in range(nz):
        cross(k).wait_send()
    for way in WAYS:
        hop(way, far, way).wait_send()
        for dist in range(1, far):
            for h in WAYS:
                hop(way, dist, h).wait_send()


def combine_call(acc, moe, h, nr, ne, runs):
    s, d = h.shape
    nz = ne // 2
    rows = acc.shape[0] // ne
    dma = pltpu.SemaphoreType.DMA
    vmem = pl.BlockSpec(memory_space=pltpu.VMEM)
    sums = pltpu.VMEM((nz, rows, LANES), jnp.float32)
    hops, back = dma((2, nz, 2)), dma((len(runs), len(QUAD)))
    return pl.pallas_call(
        functools.partial(combine_kernel, nr=nr, ne=ne, runs=runs),
        out_shape=jax.ShapeDtypeStruct((s, d), jnp.bfloat16),
        in_specs=[pl.BlockSpec(memory_space=pl.ANY), vmem, vmem],
        out_specs=vmem,
        scratch_shapes=[
            sums, sums, pltpu.VMEM((2, nz // 2, rows, LANES), jnp.float32),
            pltpu.VMEM((len(QUAD), sum(runs), d), jnp.bfloat16),
            *[dma((nz,))] * 3, hops, hops, back, back,
        ],
        compiler_params=pltpu.CompilerParams(collective_id=1, has_side_effects=True, vmem_limit_bytes=48 * 2**20),
        cost_estimate=pl.CostEstimate(flops=100 * 10**9, bytes_accessed=30 * 10**6, transcendentals=10**6),
        name='combine',
    )(acc, moe, h)


def router(h, wr, ids):
    r = rmsnorm(h)
    logits = jnp.dot(r, wr, precision=lax.Precision.HIGHEST, preferred_element_type=jnp.float32)
    hot = ids[:, :, None] == jnp.arange(wr.shape[1], dtype=jnp.int32)
    picked = jnp.sum(jnp.where(hot, logits[:, None, :], 0.0), axis=-1)
    return jax.nn.softmax(picked, axis=-1)


def solution(mesh):
    nr, nd = mesh.shape['replica'], mesh.shape['ep']
    side = math.isqrt(nr)
    tok, split = P(('replica', 'ep')), P('ep')

    def local(x, wq, wk, wv, wo, wr, w1, w3, w2, idx):
        b, s, d = x.shape
        t, k, ne = b * s, idx.shape[-1], w1.shape[0]
        me = lax.axis_index('ep')
        rep = lax.axis_index('replica')
        quart = t // 4
        runs = tuple(n * quart // 64 for n in RUNS)
        h, us, ids = attention_call(x.reshape(t, d), idx.reshape(t, k).T, wq, wk, wv, wo, nr, nd, runs)
        us = [lax.all_gather(u, 'ep', axis=0, tiled=True) for u in us]
        mine = 2 * (rep // side % 2) + rep % side % 2
        ids = lax.dynamic_slice_in_dim(ids.transpose(0, 2, 1), mine * quart, quart, axis=1).reshape(t, k)
        g = router(h, wr, ids)
        gi = lax.all_gather(jnp.concatenate([g, ids.astype(jnp.float32)], axis=1), 'ep', axis=0, tiled=False)
        gi = gi.reshape(nd, 4, quart, 2 * k)
        eids = me * ne + jnp.arange(ne)
        first = 0
        for u, run in zip(us, runs):
            part = gi[:, :, first:first + run].transpose(1, 0, 2, 3).reshape(-1, 2 * k)
            acc = expert_call(u, *plan(part[:, k:].astype(jnp.int32), part[:, :k], eids, d), w1, w3, w2, run)
            first += run
            if first < quart:
                moe = lax.psum_scatter(acc, 'ep', scatter_dimension=0, tiled=True)
        return combine_call(acc, moe, h, nr, nd, runs).reshape(b, s, d)

    return jax.shard_map(local, mesh=mesh,
                         in_specs=(tok, split, split, split, split, P(), split, split, split, tok),
                         out_specs=tok, check_vma=False)
```

time: 7660 us -> 470 us (0.06); the launches traced: 7560 us -> 466 us
  blocking collectives: 5080 us -> 18.8 us
  local copies, waits for them, and re-layouts: 956 us -> 9.65 us
  other arithmetic: 736 us -> 13.4 us
  loops' own time: 389 us -> 0 us
  Pallas kernels: 0 us -> 349 us
  waiting for transfers between devices: 230 us -> 57.1 us
  matrix products: 138 us -> 3.81 us
    all_to_all x1 -> x0, blocking collectives: 5080 us -> none  [a2a(): return lax.all_to_all(v, 'ep', 0, 0, tiled=True)]
    scatter-add x17 -> x0, other arithmetic: 635 us -> none  [the longest x15 355 us: work(): return acc.at[rb].add(gb[:, None] * o.astype(jnp.float32))]
    gather x32 -> x0, local copies, waits for them, and re-layouts: 568 us -> none  [the longest x1 186 us: expert_sum(): gate = jnp.where(ok, gates[jnp.minimum(cand, m - 1)], 0.0)]
    another operation x266 -> x0, loops' own time: 389 us -> none  [the longest x1 360 us: expert_sum(): lax.scan(body, jnp.zeros((n, d), jnp.float32), (jnp.arange(cand.shape[0])...]
    pallas_call x0 -> x4, Pallas kernels: none -> 349 us  [the longest x1 141 us: attention_call(): pl.pallas_call(functools.partial(attention_kernel, nr=nr, ne=ne, runs=run...]
    all_gather x4 -> x2, waiting for transfers between devices: 227 us -> 13.1 us  [local(): us = [lax.all_gather(u, 'ep', axis=0, tiled=True) for u in us]]
    dynamic_slice x279 -> x2, local copies, waits for them, and re-layouts: 164 us -> 0.8 us  [local(): lax.dynamic_slice_in_dim(ids.transpose(0, 2, 1), mine * quart, quart, axi...]
    dot_general x35 -> x4, matrix products: 136 us -> 0.66 us  [the longest x2 0.42 us: plan(): jnp.einsum('ij,bje->bie', ahead(LANES), spb, preferred_element_type=jnp.f...]
  transfers between devices with their start and end apart: 7 -> 3, of which waited for: 4 -> 2; matrix products, arithmetic and copies ran while one was open for 13% -> 5% of each run, Pallas kernels for 0% -> 24%
where the time goes in v2:
time: 470 us; the launch traced here: 466 us
  Pallas kernels  349 us (74%)
  waiting for transfers between devices  57.1 us (12%)
  blocking collectives  18.8 us (4%)
  between operations  13.5 us (3%)
  other arithmetic  13.4 us (3%)
  local copies, waits for them, and re-layouts  9.65 us (2%)
    pallas_call x1, Pallas kernels, attention_call(): pl.pallas_call(functools.partial(attention_kernel, nr=nr, ne=ne, runs=run...  141 us
    pallas_call x2, Pallas kernels, expert_call(): pl.pallas_call(functools.partial(expert_kernel, cap=cap, run=run), out_sh...  113 us
    pallas_call x1, Pallas kernels, combine_call(): pl.pallas_call(functools.partial(combine_kernel, nr=nr, ne=ne, runs=runs)...  94.6 us
    reduce_scatter x1, waiting for transfers between devices, local(): moe = lax.psum_scatter(acc, 'ep', scatter_dimension=0, tiled=True)  43.2 us
    all_gather x1, blocking collectives, local(): lax.all_gather(jnp.concatenate([g, ids.astype(jnp.float32)], axis=1), 'ep...  18.8 us
    all_gather x2, waiting for transfers between devices, local(): us = [lax.all_gather(u, 'ep', axis=0, tiled=True) for u in us]  13.1 us
  transfers between devices with their start and end apart: 3, of which 2 were waited for; matrix products, arithmetic and copies ran while one was open for 5% of the time, Pallas kernels for 24%

profile of v2, /device:TPU:21, one launch (start us, length us, event | category | flops | bytes accessed | tf_op | source)
XLA Modules:
  0.0 465.9 jit_solution(9259291011789483141)
XLA Ops:
  6.6 141.4 %attention.1 = (bf16[256,2048]{1,0:T(8,128)(2,1)}, s32[4,8,256]{2,1,0:T(8,128)}, bf16[128,2048]{1,0:T(8,128)(2,1)}, bf16[128,2048]{1,0:T(8,128)(2,1)}) custom-call(bf16[256,2048]{1,0:T(8,128)(2,1)} %bitcast.107, s32[8,256]{1,0:T(8,128)} %bitcast.108, bf16[128,4096]{1,0:T(8,128)(2,1)} %wq_hbm.1, bf16[128,4096]{1,0:T(8,128)(2,1)} %wk_hbm.1, ...), custom_call_target="tpu_custom_call" | custom-call | flops 99999997952 | bytes 30000000 | tf_op jit(solution)/shard_map/attention/pallas_call | solution.py:363
  148.1 0.7 all-gather.4.cloned.1.call-update
  149.0 0.8 dynamic-slice_bitcast_fusion
  149.8 0.1 eq.37
  149.8 0.1 copy.67
  150.0 1.5 fusion
  151.5 3.1 fusion.1
  154.7 0.9 select_reduce_fusion.4
  155.6 0.1 reduce_max.9
  155.8 18.8 %all-gather = f32[4096,16]{0,1:T(8,128)S(1)} all-gather(f32[256,16]{0,1:T(8,128)S(1)} %pad_maximum_fusion), channel_id=2, replica_groups=mesh['replica'=4,'ep'=16] {'ep'}, dimensions={0}, use_global_device_ids=true | all-gather | bytes 278528 | tf_op jit(solution)/shard_map/all_gather | solution.py:810
  174.6 0.3 reshape.111
  175.0 0.3 fusion.34
  175.3 0.1 copy_bitcast_fusion
  175.4 0.2 reshape.112
  175.6 0.2 reshape.115
  175.9 0.2 compare_reduce_fusion
  176.2 0.2 reduce_sum.144
  176.4 0.2 convert_reduce_fusion
  176.6 0.2 fusion.12
  176.8 0.1 fusion.30
  176.9 0.1 broadcast_in_dim.121
  177.0 0.2 fusion.5
  177.2 2.1 select_reduce_fusion
  179.3 0.6 copy.82
  179.9 0.2 reduce_sum.138
  180.2 0.2 convert_reduce_fusion.2
  180.4 0.1 fusion.31
  180.5 0.1 broadcast_in_dim.110
  180.6 0.2 fusion.9
  180.8 4.1 select_reduce_fusion.1
  184.9 0.6 copy.81
  185.5 0.1 copy.73
  185.5 0.6 reshape.122.dense_ref
  186.1 0.7 convert_reduce_fusion.1.nsp_ref
  186.9 13.1 %all-gather.6.cloned.1.call-done.u_hbm = bf16[2048,2048]{1,0:T(8,128)(2,1)} async-done(((bf16[128,2048]{1,0:T(8,128)(2,1)}), bf16[2048,2048]{1,0:T(8,128)(2,1)}) %all-gather.6.cloned.1.call-update) | async-done | bytes 8388624 | tf_op jit(solution)/shard_map/all_gather | solution.py:806
  199.9 56.8 %experts.3 = f32[32768,128]{1,0:T(8,128)} custom-call(s32[8]{0:T(128)} %convert_reduce_fusion.1.nsp_ref, s32[64]{0:T(128)} %reshape.122.dense_ref, s32[2048]{0:T(1024)} %bitcast.105, f32[2048]{0:T(1024)} %bitcast.103, f32[8,8,256]{2,1,0:T(8,128)} %bitcast.96, bf16[2048,2048]{1,0:T(8,128)(2,1)} %all-gather.6.cloned.1.call-done.u_hbm, ...), custom_call_target="tpu_custom_call" | custom-call | flops 60000002048 | bytes 160000000 | tf_op jit(solution)/shard_map/experts/pallas_call | solution.py:561
  256.8 2.1 select_reduce_fusion.2
  258.9 0.6 copy.80
  259.5 0.6 copy.79
  260.1 0.1 copy.70
  260.1 0.6 reshape.120.dense_ref
  260.7 0.7 convert_reduce_fusion.3.nsp_ref
  261.4 56.6 %experts.2.acc_hbm = f32[32768,128]{1,0:T(8,128)} custom-call(s32[8]{0:T(128)} %convert_reduce_fusion.3.nsp_ref, s32[64]{0:T(128)} %reshape.120.dense_ref, s32[2048]{0:T(1024)} %bitcast.106, f32[2048]{0:T(1024)} %bitcast.104, f32[8,8,256]{2,1,0:T(8,128)} %bitcast.94, bf16[2048,2048]{1,0:T(8,128)(2,1)} %all-gather.4.cloned.1.call-done.u_hbm, ...), custom_call_target="tpu_custom_call" | custom-call | flops 60000002048 | bytes 160000000 | tf_op jit(solution)/shard_map/experts/pallas_call | solution.py:561
  318.1 43.2 %reduce-scatter.2.cloned.1.call-done.moe_ref = f32[2048,128]{1,0:T(8,128)} async-done(((f32[32768,128]{1,0:T(8,128)}), f32[2048,128]{1,0:T(8,128)}) %reduce-scatter.2.cloned.1.call-update) | async-done | bytes 1048592 | tf_op jit(solution)/shard_map/reduce_scatter | solution.py:819
  361.3 1.2 copy-done
  362.5 1.2 copy-done.1
  363.7 94.6 %combine.1 = bf16[256,2048]{1,0:T(8,128)(2,1)S(1)} custom-call(f32[32768,128]{1,0:T(8,128)} %experts.2.acc_hbm, f32[2048,128]{1,0:T(8,128)S(1)} %copy-done.1, bf16[256,2048]{1,0:T(8,128)(2,1)S(1)} %copy-done), custom_call_target="tpu_custom_call" | custom-call | flops 99999997952 | bytes 30000000 | tf_op jit(solution)/shard_map/combine/pallas_call | solution.py:769
  458.4 1.0 copy.86
  (37 shorter events, 0.5 us)
Async XLA Ops:
  6.5 193.4 %all-gather.6.cloned.1.call-start = ((), (), s32[]{:S(2)}) async-start(), calls=%async_computation.2 | async-start | bytes 8912896 | tf_op jit(solution)/shard_map/all_gather | solution.py:806
  6.6 145.0 %copy-start.2 = (f32[2048,128]{1,0:T(8,128)S(1)}, f32[2048,128]{1,0:T(8,128)}, u32[]{:S(2)}) copy-start(f32[2048,128]{1,0:T(8,128)} %param.17) | copy-start | bytes 3145732
  148.0 113.4 %all-gather.4.cloned.1.call-start = ((), (), s32[]{:S(2)}) async-start(), calls=%async_computation.1 | async-start | bytes 8912896 | tf_op jit(solution)/shard_map/all_gather | solution.py:806
  148.8 212.5 %reduce-scatter.2.cloned.1.call-start = ((), (), s32[]{:S(2)}) async-start(), calls=%async_computation.3 | async-start | bytes 17825792 | tf_op jit(solution)/shard_map/reduce_scatter | solution.py:819
  176.8 23.1 %copy-start.4 = (f32[2048,8]{0,1:T(8,128)}, f32[2048,8]{0,1:T(8,128)S(1)}, u32[]{:S(2)}) copy-start(f32[2048,8]{0,1:T(8,128)S(1)} %get-tuple-element.15) | copy-start | bytes 196612
  176.8 80.0 %copy-start.3 = (f32[2048,8]{0,1:T(8,128)}, f32[2048,8]{0,1:T(8,128)S(1)}, u32[]{:S(2)}) copy-start(f32[2048,8]{0,1:T(8,128)S(1)} %get-tuple-element.16) | copy-start | bytes 196612
  361.3 1.2 copy-start
  362.5 1.2 copy-start.1
Sparse Core Ops, SparseCore 0:
  148.1 51.7 all-gather.5
  201.5 51.0 all-gather.3
  256.9 104.3 reduce-scatter.1
